TPU v7x, 32 devices: a whole 2x2x4 slice. The times are simulated.
32 devices in a mesh: rows: 8 (over y, x, core), cols: 4 (over z).
Axes of the slice: x: 2, y: 2, z: 4, core: 2. Of those that a mesh axis runs over, the one named last changes fastest.
Arguments:
- surface_field: float32 [4096, 8192], P('rows', 'cols'), may hold values from -20 to 30
- land_words: int32 [4096, 256], P('rows', 'cols'), may hold values from -2147483648 to 2147483646
Outputs:
- level_one: float32 [2048, 4096], P('rows', 'cols')
- level_two: float32 [1024, 2048], P('rows', 'cols')
- level_three: float32 [512, 1024], P('rows', 'cols')
- level_four: float32 [256, 512], P('rows', 'cols')
- level_means: float32 [4], replicated
- level_maxima: float32 [4], replicated
All inputs are finite; a program needn't handle non-finite values.
Results may differ from a plain program's by a relative error of at most 0.0001.
Values sent between devices are 32-bit elements; how exact they have to be, the bound alone decides.
A program may use at most 128 MiB of HBM per device.

v0:
```python
import functools
import math

import jax
import jax.numpy as jnp
from jax import lax
from jax.experimental import pallas as pl
from jax.experimental.pallas import tpu as pltpu
from jax.sharding import PartitionSpec as P

stencil_weights = (0.125, 0.375, 0.375, 0.125)
floor_value = 0.05
mean_eps = 1e-06
LEVELS = 4
LANES = 128
HALO = 16
MESH = pl.DeviceIdType.MESH


def kernel(
    row_devices,
    col_devices,
    field,
    land,
    level_one,
    level_two,
    level_three,
    level_four,
    means_ref,
    maxima_ref,
    fine,
    words,
    cosines,
    send_left,
    send_right,
    from_left,
    from_right,
    rows_top,
    rows_bottom,
    land_top,
    land_bottom,
    p0,
    c0,
    p1,
    c1,
    p2,
    c2,
    p3,
    c3,
    split,
    stat_own,
    stat_all,
    load_sem,
    halo_send,
    halo_recv,
    stat_send,
    stat_recv,
):
    rows, cols = field.shape
    tiles = cols // LANES
    count_words = land.shape[0]
    row_at = lax.axis_index("rows")
    col_at = lax.axis_index("cols")
    total_rows = rows * row_devices

    def device(down, right):
        return (
            lax.rem(row_at + down + row_devices, row_devices),
            lax.rem(col_at + right + col_devices, col_devices),
        )

    others = [
        (down, right)
        for down in range(row_devices)
        for right in range(col_devices)
        if (down, right) != (0, 0)
    ]

    def load(tile):
        start = tile * LANES
        if not isinstance(tile, int):
            start = pl.multiple_of(start, LANES)
        return pltpu.make_async_copy(
            field.at[:, pl.ds(start, LANES)], fine.at[tile], load_sem.at[tile]
        )

    load(0).start()
    load(tiles - 1).start()
    for tile in range(1, tiles - 1):
        load(tile).start()

    barrier = pltpu.get_barrier_semaphore()
    for down, right in others:
        pl.semaphore_signal(barrier, inc=1, device_id=device(down, right), device_id_type=MESH)

    def upright(array):
        if count_words < LANES:
            filler = jnp.zeros((LANES - count_words, array.shape[1]), jnp.int32)
            array = jnp.concatenate([array, filler], axis=0)
        return jnp.transpose(array)

    words[HALO : HALO + rows, :] = upright(land[...])
    lane = lax.broadcasted_iota(jnp.int32, (8, LANES), 1)

    def flags(tile, start, count):
        lanes = lax.broadcasted_iota(jnp.int32, (count, LANES), 1)
        place = tile * (LANES // 32) + lax.shift_right_logical(lanes, 5)
        word = jnp.take_along_axis(
            words[pl.ds(start, count), :], place, axis=1, mode="promise_in_bounds"
        )
        return jnp.bitwise_and(
            lax.shift_right_logical(word, jnp.bitwise_and(lanes, 31)), 1
        ).astype(jnp.float32)

    blocks = -(-(rows + 2 * HALO) // LANES)
    packed = (8 * (-(-blocks // 8)), LANES)
    row_index = (
        row_at * rows
        - HALO
        + lax.broadcasted_iota(jnp.int32, packed, 0) * LANES
        + lax.broadcasted_iota(jnp.int32, packed, 1)
    )
    latitude = ((row_index.astype(jnp.float32) + 0.5) / total_rows - 0.5) * math.pi
    on_globe = jnp.logical_and(row_index >= 0, row_index < total_rows)
    packed_cosines = jnp.where(on_globe, jnp.cos(latitude), 0.0)
    for block in range(blocks):
        size = min(LANES, rows + 2 * HALO - block * LANES)
        spread = jnp.broadcast_to(packed_cosines[block : block + 1, :], (LANES, LANES))
        cosines[block * LANES : block * LANES + size, :] = jnp.transpose(spread)[0:size, :]

    load(0).wait()
    send_left[0:HALO, :] = jnp.transpose(fine[0])[0:HALO, :]
    send_left[HALO:, :] = jnp.transpose(flags(0, HALO, rows))[0:HALO, :]
    load(tiles - 1).wait()
    send_right[0:HALO, :] = jnp.transpose(fine[tiles - 1])[LANES - HALO :, :]
    send_right[HALO:, :] = jnp.transpose(flags(tiles - 1, HALO, rows))[LANES - HALO :, :]

    zero_pad = ((p0, c0, 8), (p1, c1, 16), (p2, c2, 16), (p3, c3, 16))
    for product, cover, width in zero_pad:
        for ref in (product, cover):
            shape = (ref.shape[0], width, LANES)
            ref[:, 0:width, :] = jnp.zeros(shape, jnp.float32)
            ref[:, ref.shape[1] - width :, :] = jnp.zeros(shape, jnp.float32)

    pl.semaphore_wait(barrier, len(others))
    plan = (
        (field.at[rows - HALO : rows, :], rows_top, (1, 0)),
        (field.at[0:HALO, :], rows_bottom, (-1, 0)),
        (land.at[:, rows - LANES : rows], land_top, (1, 0)),
        (land.at[:, 0:LANES], land_bottom, (-1, 0)),
        (send_left, from_right.at[:, LANES : LANES + rows], (0, -1)),
        (send_right, from_left.at[:, LANES : LANES + rows], (0, 1)),
        (send_left.at[:, 0:LANES], from_right.at[:, LANES + rows :], (-1, -1)),
        (send_right.at[:, 0:LANES], from_left.at[:, LANES + rows :], (-1, 1)),
        (send_left.at[:, rows - LANES :], from_right.at[:, 0:LANES], (1, -1)),
        (send_right.at[:, rows - LANES :], from_left.at[:, 0:LANES], (1, 1)),
    )
    copies = []
    for place, (source, target, (down, right)) in enumerate(plan):
        copy = pltpu.make_async_remote_copy(
            src_ref=source,
            dst_ref=target,
            send_sem=halo_send.at[place],
            recv_sem=halo_recv.at[place],
            device_id=device(down, right),
            device_id_type=MESH,
        )
        copy.start()
        copies.append(copy)

    def own_tile(tile):
        for start in range(0, rows, 64):
            cover = flags(tile, HALO + start, 64) * cosines[HALO + start : HALO + start + 64, :]
            c0[tile + 1, 24 + start : 88 + start, :] = cover
            p0[tile + 1, 24 + start : 88 + start, :] = cover * fine[tile, start : start + 64, :]

    own_tile(0)
    own_tile(tiles - 1)

    @pl.loop(1, tiles - 1)
    def _(tile):
        load(tile).wait()
        own_tile(tile)

    for copy in copies:
        copy.wait()

    words[0:HALO, :] = upright(land_top[...])[LANES - HALO :, :]
    words[HALO + rows :, :] = upright(land_bottom[...])[0:HALO, :]
    for landed, at in ((rows_top, 0), (rows_bottom, HALO + rows)):
        for tile in range(tiles):
            cover = flags(tile, at, HALO) * cosines[at : at + HALO, :]
            c0[tile + 1, 8 + at : 8 + at + HALO, :] = cover
            p0[tile + 1, 8 + at : 8 + at + HALO, :] = (
                cover * landed[:, tile * LANES : (tile + 1) * LANES]
            )
    filler = jnp.zeros((LANES - HALO, rows + 2 * LANES), jnp.float32)
    first = LANES - HALO
    last = LANES + rows + HALO
    for packet, tile, at_end in ((from_left, 0, True), (from_right, tiles + 1, False)):
        sides = []
        for part in (packet[0:HALO, :], packet[HALO:, :]):
            pieces = [filler, part] if at_end else [part, filler]
            sides.append(jnp.transpose(jnp.concatenate(pieces, axis=0))[first:last, :])
        cover = sides[1] * cosines[...]
        c0[tile, 8 : 8 + rows + 2 * HALO, :] = cover
        p0[tile, 8 : 8 + rows + 2 * HALO, :] = cover * sides[0]

    band_row = lax.broadcasted_iota(jnp.int32, (4 * LANES, LANES), 0)
    band_col = lax.broadcasted_iota(jnp.int32, (4 * LANES, LANES), 1)
    tap = band_row - (LANES - 1) - 2 * band_col
    band = jnp.where(
        jnp.logical_or(tap == 0, tap == 3),
        stencil_weights[0],
        jnp.where(jnp.logical_or(tap == 1, tap == 2), stencil_weights[1], 0.0),
    ).astype(jnp.bfloat16)

    stats = []
    sources = ((p0, c0), (p1, c1), (p2, c2), (p3, c3))
    outputs = (level_one, level_two, level_three, level_four)
    for level in range(LEVELS):
        product_in, cover_in = sources[level]
        output = outputs[level]
        own = output.shape[0]
        count = own + 16
        tiles_in = product_in.shape[0]
        tiles_out = output.shape[1] // LANES

        @pl.loop(0, tiles_in)
        def _(tile):
            offset = pl.multiple_of(tile * LANES, LANES)
            for place, ref in enumerate((product_in, cover_in)):
                taps = [ref[tile, pl.ds(7 + a, count, stride=2), :] for a in range(4)]
                down = stencil_weights[0] * (taps[0] + taps[3]) + stencil_weights[1] * (
                    taps[1] + taps[2]
                )
                high = down.astype(jnp.bfloat16)
                low = (down - high.astype(jnp.float32)).astype(jnp.bfloat16)
                at = 2 * place * count
                split[at : at + count, pl.ds(offset, LANES)] = high
                split[at + count : at + 2 * count, pl.ds(offset, LANES)] = low

        index = row_at * own - 8 + lax.broadcasted_iota(jnp.int32, (count, LANES), 0)
        inside = jnp.logical_and(index >= 0, index < own * row_devices)

        def across(start, width, table):
            result = jnp.dot(
                split[0 : 4 * count, pl.ds(start, width)],
                table,
                preferred_element_type=jnp.float32,
            )
            num = result[0:count] + result[count : 2 * count]
            den = result[2 * count : 3 * count] + result[3 * count :]
            value = num / jnp.maximum(den, floor_value)
            cover = jnp.where(inside, den, 0.0)
            return value, cover, cover * value

        def keep(tile, cover, product):
            if level + 1 < LEVELS:
                product_out, cover_out = sources[level + 1]
                product_out[tile, 16 : 16 + count, :] = product
                cover_out[tile, 16 : 16 + count, :] = cover

        if level + 1 < LEVELS:
            value, cover, product = across(0, 2 * LANES, band[2 * LANES :])
            keep(0, cover, product)
            value, cover, product = across((tiles_in - 2) * LANES, 2 * LANES, band[: 2 * LANES])
            keep(tiles_out + 1, cover, product)

        def own_columns(tile, carry):
            weighted, total, largest = carry
            value, cover, product = across(
                pl.multiple_of(tile * 2 * LANES, 2 * LANES), 4 * LANES, band
            )
            keep(tile + 1, cover, product)
            output[:, pl.ds(pl.multiple_of(tile * LANES, LANES), LANES)] = value[8 : 8 + own]

            def parts(array):
                return array[8 : 8 + own].reshape(own // 8, 8, LANES)

            return (
                weighted + jnp.sum(parts(product), axis=0),
                total + jnp.sum(parts(cover), axis=0),
                jnp.maximum(largest, jnp.max(parts(value), axis=0)),
            )

        zero = jnp.zeros((8, LANES), jnp.float32)
        start = (zero, zero, jnp.full((8, LANES), -jnp.inf, jnp.float32))
        stats.append(lax.fori_loop(0, tiles_out, own_columns, start))

    row = lax.broadcasted_iota(jnp.int32, (8, LANES), 0)
    gathered = []
    for kind, reduce in ((0, jnp.sum), (1, jnp.sum), (2, jnp.max)):
        tile = jnp.zeros((8, LANES), jnp.float32)
        for level in range(LEVELS):
            tile = jnp.where(row == level, reduce(stats[level][kind], axis=0, keepdims=True), tile)
        gathered.append(reduce(tile, axis=1, keepdims=True))
    stat_own[...] = jnp.where(
        lane == 0, gathered[0], jnp.where(lane == 1, gathered[1], gathered[2])
    )
    copies = []
    for place, (down, right) in enumerate(others):
        copy = pltpu.make_async_remote_copy(
            src_ref=stat_own,
            dst_ref=stat_all.at[place],
            send_sem=stat_send.at[place],
            recv_sem=stat_recv.at[place],
            device_id=device(down, right),
            device_id_type=MESH,
        )
        copy.start()
        copies.append(copy)
    for copy in copies:
        copy.wait()
    summed = stat_own[...] + jnp.sum(stat_all[...], axis=0)
    largest = jnp.maximum(stat_own[...], jnp.max(stat_all[...], axis=0))
    weighted = jnp.sum(jnp.where(lane == 0, summed, 0.0), axis=1, keepdims=True)
    total = jnp.sum(jnp.where(lane == 1, summed, 0.0), axis=1, keepdims=True)
    level_means = jnp.broadcast_to(weighted / (total + mean_eps), (8, LANES))
    for level in range(LEVELS):
        here = jnp.logical_and(row == level, lane == 2)
        means_ref[level] = jnp.sum(jnp.where(here, level_means, 0.0))
        maxima_ref[level] = jnp.sum(jnp.where(here, largest, 0.0))


def per_device(row_devices, col_devices, surface_field, land_words):
    rows, cols = surface_field.shape
    f32 = jnp.float32
    levels = tuple(
        jax.ShapeDtypeStruct((rows >> level, cols >> level), f32) for level in range(1, LEVELS + 1)
    )
    scratch = [
        pltpu.VMEM((cols // LANES, rows, LANES), f32),
        pltpu.VMEM((rows + 2 * HALO, LANES), jnp.int32),
        pltpu.VMEM((rows + 2 * HALO, LANES), f32),
        pltpu.VMEM((2 * HALO, rows), f32),
        pltpu.VMEM((2 * HALO, rows), f32),
        pltpu.VMEM((2 * HALO, rows + 2 * LANES), f32),
        pltpu.VMEM((2 * HALO, rows + 2 * LANES), f32),
        pltpu.VMEM((HALO, cols), f32),
        pltpu.VMEM((HALO, cols), f32),
        pltpu.VMEM((land_words.shape[1], LANES), jnp.int32),
        pltpu.VMEM((land_words.shape[1], LANES), jnp.int32),
    ]
    for level in range(LEVELS):
        shape = ((cols >> level) // LANES + 2, (rows >> level) + 48, LANES)
        scratch += [pltpu.VMEM(shape, f32)] * 2
    others = row_devices * col_devices - 1
    scratch += [
        pltpu.VMEM((4 * (rows // 2 + 16), cols + 2 * LANES), jnp.bfloat16),
        pltpu.VMEM((8, LANES), f32),
        pltpu.VMEM((others, 8, LANES), f32),
        pltpu.SemaphoreType.DMA((cols // LANES,)),
        pltpu.SemaphoreType.DMA((10,)),
        pltpu.SemaphoreType.DMA((10,)),
        pltpu.SemaphoreType.DMA((others,)),
        pltpu.SemaphoreType.DMA((others,)),
    ]
    vmem = pl.BlockSpec(memory_space=pltpu.VMEM)
    smem = pl.BlockSpec(memory_space=pltpu.SMEM)
    small = jax.ShapeDtypeStruct((LEVELS,), f32)
    found = pl.pallas_call(
        functools.partial(kernel, row_devices, col_devices),
        out_shape=(*levels, small, small),
        in_specs=[pl.BlockSpec(memory_space=pl.ANY), vmem],
        out_specs=(vmem, vmem, vmem, vmem, smem, smem),
        scratch_shapes=scratch,
        compiler_params=pltpu.CompilerParams(
            collective_id=0, has_side_effects=True, vmem_limit_bytes=60 * 1024 * 1024
        ),
        name="coarsen_levels",
    )(surface_field, land_words.T)

    any_place = pl.BlockSpec(memory_space=pl.ANY)
    return pl.pallas_call(
        hand_over,
        out_shape=(*levels, small, small),
        in_specs=[vmem] * LEVELS + [smem] * 2,
        out_specs=(any_place,) * LEVELS + (smem,) * 2,
        scratch_shapes=[pltpu.SemaphoreType.DMA((LEVELS,))],
        name="hand_over",
    )(*found)


def hand_over(*refs):
    count = LEVELS + 2
    sources, targets, sems = refs[:count], refs[count : 2 * count], refs[2 * count]
    copies = [
        pltpu.make_async_copy(sources[at], targets[at], sems.at[at]) for at in range(LEVELS)
    ]
    for copy in copies:
        copy.start()
    for at in range(LEVELS):
        targets[LEVELS][at] = sources[LEVELS][at]
        targets[LEVELS + 1][at] = sources[LEVELS + 1][at]
    for copy in copies:
        copy.wait()


def solution(mesh):
    return jax.shard_map(
        functools.partial(per_device, mesh.shape["rows"], mesh.shape["cols"]),
        mesh=mesh,
        in_specs=(P("rows", "cols"), P("rows", "cols")),
        out_specs=(
            P("rows", "cols"),
            P("rows", "cols"),
            P("rows", "cols"),
            P("rows", "cols"),
            P(),
            P(),
        ),
        check_vma=False,
    )
```

profile of v0, /device:TPU:0, one launch (start us, length us, event | category | flops | bytes accessed | tf_op | source)
XLA Modules:
  0.0 36.0 jit_solution(13046896485505965411)
XLA Ops:
  0.6 32.4 %coarsen_levels.1 = (f32[256,1024]{1,0:T(8,128)}, f32[128,512]{1,0:T(8,128)}, f32[64,256]{1,0:T(8,128)}, f32[32,128]{1,0:T(8,128)}, f32[4]{0:T(128)}, /*index=5*/f32[4]{0:T(128)}) custom-call(f32[512,2048]{1,0:T(8,128)} %field.1, s32[64,512]{1,0:T(8,128)} %bitcast.1), custom_call_target="tpu_custom_call" | custom-call | tf_op jit(solution)/shard_map/coarsen_levels/pallas_call | solution.py:362
  33.0 3.0 %hand_over.1 = (f32[256,1024]{1,0:T(8,128)}, f32[128,512]{1,0:T(8,128)}, f32[64,256]{1,0:T(8,128)}, f32[32,128]{1,0:T(8,128)}, f32[4]{0:T(128)}, /*index=5*/f32[4]{0:T(128)}) custom-call(f32[256,1024]{1,0:T(8,128)} %get-tuple-element.12.refs_0_, f32[128,512]{1,0:T(8,128)} %get-tuple-element.13.refs_1_, f32[64,256]{1,0:T(8,128)} %get-tuple-element.14.refs_2_, ...), custom_call_target="tpu_custom_call" | custom-call | tf_op jit(solution)/shard_map/hand_over/pallas_call | solution.py:375
where the time goes:
time: 36.2 us; the launch traced here: 36 us
  Pallas kernels  35.4 us (98%)
  between operations  0.64 us (2%)
    pallas_call x1, Pallas kernels, per_device(): pl.pallas_call(functools.partial(kernel, row_devices, col_devices), out_s...  32.4 us
    pallas_call x1, Pallas kernels, per_device(): pl.pallas_call(hand_over, out_shape=(*levels, small, small), in_specs=[vm...  2.95 us

commit v1 on v0

--- a/solution.py
+++ b/solution.py
@@ -21,13 +21,14 @@
     row_devices,
     col_devices,
     field,
-    land,
+    land_words,
     level_one,
     level_two,
     level_three,
     level_four,
     means_ref,
     maxima_ref,
+    land,
     fine,
     words,
     cosines,
@@ -51,6 +52,7 @@
     stat_own,
     stat_all,
     load_sem,
+    land_sem,
     halo_send,
     halo_recv,
     stat_send,
@@ -58,7 +60,7 @@
 ):
     rows, cols = field.shape
     tiles = cols // LANES
-    count_words = land.shape[0]
+    count_words = land_words.shape[0]
     row_at = lax.axis_index("rows")
     col_at = lax.axis_index("cols")
     total_rows = rows * row_devices
@@ -84,14 +86,16 @@
             field.at[:, pl.ds(start, LANES)], fine.at[tile], load_sem.at[tile]
         )
 
+    barrier = pltpu.get_barrier_semaphore()
+    for down, right in others:
+        pl.semaphore_signal(barrier, inc=1, device_id=device(down, right), device_id_type=MESH)
+
+    land_load = pltpu.make_async_copy(land_words, land, land_sem)
+    land_load.start()
     load(0).start()
     load(tiles - 1).start()
     for tile in range(1, tiles - 1):
         load(tile).start()
-
-    barrier = pltpu.get_barrier_semaphore()
-    for down, right in others:
-        pl.semaphore_signal(barrier, inc=1, device_id=device(down, right), device_id_type=MESH)
 
     def upright(array):
         if count_words < LANES:
@@ -99,6 +103,7 @@
             array = jnp.concatenate([array, filler], axis=0)
         return jnp.transpose(array)
 
+    land_load.wait()
     words[HALO : HALO + rows, :] = upright(land[...])
     lane = lax.broadcasted_iota(jnp.int32, (8, LANES), 1)
 
@@ -289,20 +294,19 @@
         stats.append(lax.fori_loop(0, tiles_out, own_columns, start))
 
     row = lax.broadcasted_iota(jnp.int32, (8, LANES), 0)
-    gathered = []
+    own = jnp.zeros((8, LANES), jnp.float32)
     for kind, reduce in ((0, jnp.sum), (1, jnp.sum), (2, jnp.max)):
         tile = jnp.zeros((8, LANES), jnp.float32)
         for level in range(LEVELS):
             tile = jnp.where(row == level, reduce(stats[level][kind], axis=0, keepdims=True), tile)
-        gathered.append(reduce(tile, axis=1, keepdims=True))
-    stat_own[...] = jnp.where(
-        lane == 0, gathered[0], jnp.where(lane == 1, gathered[1], gathered[2])
-    )
+        own = jnp.where(lane == row + kind * LEVELS, reduce(tile, axis=1, keepdims=True), own)
+    own = jnp.where(row < LEVELS, own, 0.0)
+    stat_own[...] = jnp.broadcast_to(jnp.sum(own, axis=0, keepdims=True), (8, LANES))
     copies = []
     for place, (down, right) in enumerate(others):
         copy = pltpu.make_async_remote_copy(
-            src_ref=stat_own,
-            dst_ref=stat_all.at[place],
+            src_ref=stat_own.at[0:1],
+            dst_ref=stat_all.at[place : place + 1],
             send_sem=stat_send.at[place],
             recv_sem=stat_recv.at[place],
             device_id=device(down, right),
@@ -312,15 +316,20 @@
         copies.append(copy)
     for copy in copies:
         copy.wait()
-    summed = stat_own[...] + jnp.sum(stat_all[...], axis=0)
-    largest = jnp.maximum(stat_own[...], jnp.max(stat_all[...], axis=0))
-    weighted = jnp.sum(jnp.where(lane == 0, summed, 0.0), axis=1, keepdims=True)
-    total = jnp.sum(jnp.where(lane == 1, summed, 0.0), axis=1, keepdims=True)
-    level_means = jnp.broadcast_to(weighted / (total + mean_eps), (8, LANES))
-    for level in range(LEVELS):
-        here = jnp.logical_and(row == level, lane == 2)
-        means_ref[level] = jnp.sum(jnp.where(here, level_means, 0.0))
-        maxima_ref[level] = jnp.sum(jnp.where(here, largest, 0.0))
+    first = stat_own[0:1, :]
+    summed = first + jnp.sum(stat_all[...], axis=0, keepdims=True)
+    largest = jnp.maximum(first, jnp.max(stat_all[...], axis=0, keepdims=True))
+    summed = jnp.broadcast_to(summed, (8, LANES))
+    largest = jnp.broadcast_to(largest, (8, LANES))
+
+    def pick(array, kind):
+        here = jnp.logical_and(lane == row + kind * LEVELS, row < LEVELS)
+        return jnp.sum(jnp.where(here, array, 0.0), axis=1, keepdims=True)
+
+    level_means = pick(summed, 0) / (pick(summed, 1) + mean_eps)
+    diagonal = jnp.logical_and(lane == row, row < LEVELS)
+    means_ref[...] = jnp.sum(jnp.where(diagonal, level_means, 0.0), axis=0)[0:LEVELS]
+    maxima_ref[...] = jnp.sum(jnp.where(diagonal, pick(largest, 2), 0.0), axis=0)[0:LEVELS]
 
 
 def per_device(row_devices, col_devices, surface_field, land_words):
@@ -330,6 +339,7 @@
         jax.ShapeDtypeStruct((rows >> level, cols >> level), f32) for level in range(1, LEVELS + 1)
     )
     scratch = [
+        pltpu.VMEM((land_words.shape[1], rows), jnp.int32),
         pltpu.VMEM((cols // LANES, rows, LANES), f32),
         pltpu.VMEM((rows + 2 * HALO, LANES), jnp.int32),
         pltpu.VMEM((rows + 2 * HALO, LANES), f32),
@@ -349,24 +359,24 @@
     scratch += [
         pltpu.VMEM((4 * (rows // 2 + 16), cols + 2 * LANES), jnp.bfloat16),
         pltpu.VMEM((8, LANES), f32),
-        pltpu.VMEM((others, 8, LANES), f32),
+        pltpu.VMEM((others, LANES), f32),
         pltpu.SemaphoreType.DMA((cols // LANES,)),
+        pltpu.SemaphoreType.DMA,
         pltpu.SemaphoreType.DMA((10,)),
         pltpu.SemaphoreType.DMA((10,)),
         pltpu.SemaphoreType.DMA((others,)),
         pltpu.SemaphoreType.DMA((others,)),
     ]
     vmem = pl.BlockSpec(memory_space=pltpu.VMEM)
-    smem = pl.BlockSpec(memory_space=pltpu.SMEM)
     small = jax.ShapeDtypeStruct((LEVELS,), f32)
     found = pl.pallas_call(
         functools.partial(kernel, row_devices, col_devices),
-        out_shape=(*levels, small, small),
-        in_specs=[pl.BlockSpec(memory_space=pl.ANY), vmem],
-        out_specs=(vmem, vmem, vmem, vmem, smem, smem),
+        out_shape=tuple(pltpu.VMEM(each.shape, each.dtype) for each in (*levels, small, small)),
+        in_specs=[pl.BlockSpec(memory_space=pltpu.HBM)] * 2,
+        out_specs=(vmem,) * (LEVELS + 2),
         scratch_shapes=scratch,
         compiler_params=pltpu.CompilerParams(
-            collective_id=0, has_side_effects=True, vmem_limit_bytes=60 * 1024 * 1024
+            collective_id=0, has_side_effects=True, vmem_limit_bytes=56 * 1024 * 1024
         ),
         name="coarsen_levels",
     )(surface_field, land_words.T)
@@ -375,9 +385,10 @@
     return pl.pallas_call(
         hand_over,
         out_shape=(*levels, small, small),
-        in_specs=[vmem] * LEVELS + [smem] * 2,
-        out_specs=(any_place,) * LEVELS + (smem,) * 2,
-        scratch_shapes=[pltpu.SemaphoreType.DMA((LEVELS,))],
+        in_specs=[vmem] * (LEVELS + 2),
+        out_specs=(any_place,) * (LEVELS + 2),
+        scratch_shapes=[pltpu.SemaphoreType.DMA((LEVELS + 2,))],
+        compiler_params=pltpu.CompilerParams(vmem_limit_bytes=8 * 1024 * 1024),
         name="hand_over",
     )(*found)
 
@@ -386,13 +397,10 @@
     count = LEVELS + 2
     sources, targets, sems = refs[:count], refs[count : 2 * count], refs[2 * count]
     copies = [
-        pltpu.make_async_copy(sources[at], targets[at], sems.at[at]) for at in range(LEVELS)
+        pltpu.make_async_copy(sources[at], targets[at], sems.at[at]) for at in range(count)
     ]
     for copy in copies:
         copy.start()
-    for at in range(LEVELS):
-        targets[LEVELS][at] = sources[LEVELS][at]
-        targets[LEVELS + 1][at] = sources[LEVELS + 1][at]
     for copy in copies:
         copy.wait()
 

time: 36.2 us -> 31.4 us (0.87)
  Pallas kernels: 35.4 us -> 30.6 us
    pallas_call x1, Pallas kernels: 32.4 us -> 29.5 us  [per_device(): pl.pallas_call(functools.partial(kernel, row_devices, col_devices), out_s...]
    pallas_call x1, Pallas kernels: 2.95 us -> 1.12 us  [per_device(): pl.pallas_call(hand_over, out_shape=(*levels, small, small), in_specs=[vm...]
where the time goes in v1:
time: 31.4 us; the launch traced here: 31.2 us
  Pallas kernels  30.6 us (97%)
  between operations  0.64 us (2%)
    pallas_call x1, Pallas kernels, per_device(): pl.pallas_call(functools.partial(kernel, row_devices, col_devices), out_s...  29.5 us
    pallas_call x1, Pallas kernels, per_device(): pl.pallas_call(hand_over, out_shape=(*levels, small, small), in_specs=[vm...  1.12 us

profile of v1, /device:TPU:0, one launch (start us, length us, event | category | flops | bytes accessed | tf_op | source)
XLA Modules:
  0.0 31.2 jit_solution(4154069325520182031)
XLA Ops:
  0.6 29.5 %coarsen_levels.1 = (f32[256,1024]{1,0:T(8,128)S(1)}, f32[128,512]{1,0:T(8,128)S(1)}, f32[64,256]{1,0:T(8,128)S(1)}, f32[32,128]{1,0:T(8,128)S(1)}, f32[4]{0:T(128)S(1)}, /*index=5*/f32[4]{0:T(128)S(1)}) custom-call(f32[512,2048]{1,0:T(8,128)} %field.1, s32[64,512]{1,0:T(8,128)} %bitcast.1), custom_call_target="tpu_custom_call" | custom-call | tf_op jit(solution)/shard_map/coarsen_levels/pallas_call | solution.py:372
  30.1 1.1 %hand_over.1 = (f32[256,1024]{1,0:T(8,128)}, f32[128,512]{1,0:T(8,128)}, f32[64,256]{1,0:T(8,128)}, f32[32,128]{1,0:T(8,128)}, f32[4]{0:T(128)}, /*index=5*/f32[4]{0:T(128)}) custom-call(f32[256,1024]{1,0:T(8,128)S(1)} %get-tuple-element.12.refs_0_, f32[128,512]{1,0:T(8,128)S(1)} %get-tuple-element.13.refs_1_, f32[64,256]{1,0:T(8,128)S(1)} %get-tuple-element.14.refs_2_, ...), custom_call_target="tpu_custom_call" | custom-call | tf_op jit(solution)/shard_map/hand_over/pallas_call | solution.py:385

commit v2 on v1

v2 whole, which is shorter than its diff:
```python
import functools
import math

import jax
import jax.numpy as jnp
from jax import lax
from jax.experimental import pallas as pl
from jax.experimental.pallas import tpu as pltpu
from jax.sharding import PartitionSpec as P

stencil_weights = (0.125, 0.375, 0.375, 0.125)
floor_value = 0.05
mean_eps = 1e-06
LEVELS = 4
LANES = 128
HALO = 16
EDGE = 16
MESH = pl.DeviceIdType.MESH
f32 = jnp.float32
bf16 = jnp.bfloat16


def kernel(
    row_devices,
    col_devices,
    field,
    land_words,
    level_one,
    level_two,
    level_three,
    level_four,
    means_ref,
    maxima_ref,
    fine,
    land,
    words,
    cosines,
    cos_rows,
    send_left,
    send_right,
    side,
    side_words,
    p0,
    c0,
    p1,
    c1,
    p2,
    c2,
    p3,
    c3,
    split0,
    edge0,
    split1,
    split2,
    split3,
    stat_own,
    stat_all,
    load_sem,
    land_sem,
    halo_send,
    halo_recv,
    stat_send,
    stat_recv,
):
    rows, cols = field.shape
    tiles = cols // LANES
    count_words = land.shape[0]
    row_at = lax.axis_index("rows")
    col_at = lax.axis_index("cols")
    total_rows = rows * row_devices
    has_above = row_at > 0
    has_below = row_at < row_devices - 1

    def device(down, right):
        return (
            lax.rem(row_at + down + row_devices, row_devices),
            lax.rem(col_at + right + col_devices, col_devices),
        )

    others = [
        (down, right)
        for down in range(row_devices)
        for right in range(col_devices)
        if (down, right) != (0, 0)
    ]

    barrier = pltpu.get_barrier_semaphore()
    for down, right in others:
        pl.semaphore_signal(barrier, inc=1, device_id=device(down, right), device_id_type=MESH)

    land_load = pltpu.make_async_copy(land_words, land, land_sem)
    land_load.start()

    def load(tile):
        start = tile * LANES
        if not isinstance(tile, int):
            start = pl.multiple_of(start, LANES)
        return pltpu.make_async_copy(
            field.at[:, pl.ds(start, LANES)],
            fine.at[tile, pl.ds(HALO, rows), :],
            load_sem.at[tile],
        )

    order = [0, tiles - 1, *range(1, tiles - 1)]
    for tile in order:
        load(tile).start()

    def clear(row_start, lane_start):
        fine[:, row_start : row_start + HALO, :] = jnp.zeros((tiles, HALO, LANES), f32)
        words[row_start : row_start + HALO, :] = jnp.zeros((HALO, LANES), jnp.int32)
        here = slice(lane_start, lane_start + LANES)
        side[0:HALO, here] = jnp.zeros((HALO, LANES), f32)
        side[LANES - HALO :, here] = jnp.zeros((HALO, LANES), f32)
        side_words[:, here] = jnp.zeros((8, LANES), jnp.int32)

    @pl.when(jnp.logical_not(has_above))
    def _():
        clear(0, 0)

    @pl.when(jnp.logical_not(has_below))
    def _():
        clear(HALO + rows, LANES + rows)

    land_load.wait()
    upright = land[...]
    if count_words < LANES:
        filler = jnp.zeros((LANES - count_words, rows), jnp.int32)
        upright = jnp.concatenate([upright, filler], axis=0)
    words[HALO : HALO + rows, :] = jnp.transpose(upright)

    load(0).wait()
    send_left[...] = jnp.transpose(fine[0, HALO : HALO + rows, :])[0:HALO, :]
    load(tiles - 1).wait()
    send_right[...] = jnp.transpose(fine[tiles - 1, HALO : HALO + rows, :])[LANES - HALO :, :]
    for tile in range(1, tiles - 1):
        load(tile).wait()

    pl.semaphore_wait(barrier, len(others))

    first_words = land.at[0:1, :]
    last_words = land.at[count_words - 1 : count_words, :]
    own_lanes = pl.ds(LANES, rows)
    top_lanes = pl.ds(0, LANES)
    bottom_lanes = pl.ds(LANES + rows, LANES)
    ahead = pl.ds(0, LANES)
    behind = pl.ds(rows - LANES, LANES)
    right_side = side.at[0:HALO, :]
    left_side = side.at[LANES - HALO :, :]
    right_words = side_words.at[0:1, :]
    left_words = side_words.at[1:2, :]
    across_plan = (
        (send_left, right_side.at[:, own_lanes], (0, -1)),
        (send_right, left_side.at[:, own_lanes], (0, 1)),
        (first_words, right_words.at[:, own_lanes], (0, -1)),
        (last_words, left_words.at[:, own_lanes], (0, 1)),
    )
    down_plan = (
        (fine.at[:, rows : rows + HALO, :], fine.at[:, 0:HALO, :], (1, 0)),
        (words.at[rows : rows + HALO, :], words.at[0:HALO, :], (1, 0)),
        (send_left.at[:, behind], right_side.at[:, top_lanes], (1, -1)),
        (send_right.at[:, behind], left_side.at[:, top_lanes], (1, 1)),
        (first_words.at[:, behind], right_words.at[:, top_lanes], (1, -1)),
        (last_words.at[:, behind], left_words.at[:, top_lanes], (1, 1)),
    )
    up_plan = (
        (fine.at[:, HALO : 2 * HALO, :], fine.at[:, HALO + rows :, :], (-1, 0)),
        (words.at[HALO : 2 * HALO, :], words.at[HALO + rows :, :], (-1, 0)),
        (send_left.at[:, ahead], right_side.at[:, bottom_lanes], (-1, -1)),
        (send_right.at[:, ahead], left_side.at[:, bottom_lanes], (-1, 1)),
        (first_words.at[:, ahead], right_words.at[:, bottom_lanes], (-1, -1)),
        (last_words.at[:, ahead], left_words.at[:, bottom_lanes], (-1, 1)),
    )
    plans = (across_plan, down_plan, up_plan)
    first_slot = (0, len(across_plan), len(across_plan) + len(down_plan))

    def copies(which):
        return [
            pltpu.make_async_remote_copy(
                src_ref=source,
                dst_ref=target,
                send_sem=halo_send.at[first_slot[which] + place],
                recv_sem=halo_recv.at[first_slot[which] + place],
                device_id=device(down, right),
                device_id_type=MESH,
            )
            for place, (source, target, (down, right)) in enumerate(plans[which])
        ]

    for copy in copies(0):
        copy.start()

    @pl.when(has_below)
    def _():
        for copy in copies(1):
            copy.start()

    @pl.when(has_above)
    def _():
        for copy in copies(2):
            copy.start()

    blocks = rows // LANES + 2
    packed = cos_rows.shape
    row_index = (
        row_at * rows
        - LANES
        + lax.broadcasted_iota(jnp.int32, packed, 0) * LANES
        + lax.broadcasted_iota(jnp.int32, packed, 1)
    )
    latitude = ((row_index.astype(f32) + 0.5) / total_rows - 0.5) * math.pi
    on_globe = jnp.logical_and(row_index >= 0, row_index < total_rows)
    cos_rows[...] = jnp.where(on_globe, jnp.cos(latitude), 0.0)

    def placed(block):
        if block == 0:
            return slice(LANES - HALO, LANES), 0
        if block == blocks - 1:
            return slice(0, HALO), HALO + rows
        return slice(0, LANES), HALO + (block - 1) * LANES

    for block in range(blocks):
        taken, at = placed(block)
        spread = jnp.broadcast_to(cos_rows[block : block + 1, :], (LANES, LANES))
        cosines[at : at + taken.stop - taken.start, :] = jnp.transpose(spread)[taken, :]

    for product, cover, width in ((p0, c0, 8), (p1, c1, 16), (p2, c2, 16), (p3, c3, 16)):
        for ref in (product, cover):
            shape = (ref.shape[0], width, LANES)
            ref[:, 0:width, :] = jnp.zeros(shape, f32)
            ref[:, ref.shape[1] - width :, :] = jnp.zeros(shape, f32)

    def decode(tile, start, count):
        lanes = lax.broadcasted_iota(jnp.int32, (count, LANES), 1)
        place = tile * (LANES // 32) + lax.shift_right_logical(lanes, 5)
        word = jnp.take_along_axis(
            words[pl.ds(start, count), :], place, axis=1, mode="promise_in_bounds"
        )
        bit = lax.shift_left(jnp.ones_like(lanes), jnp.bitwise_and(lanes, 31))
        cover = jnp.where(
            jnp.bitwise_and(word, bit) != 0, cosines[pl.ds(start, count), :], 0.0
        )
        c0[tile, pl.ds(8 + start, count), :] = cover
        p0[tile, pl.ds(8 + start, count), :] = cover * fine[tile, pl.ds(start, count), :]

    sources = ((p0, c0), (p1, c1), (p2, c2), (p3, c3))
    outputs = (level_one, level_two, level_three, level_four)

    def downward(level, tile, first, count, target, at, stride, lanes_at):
        for place, ref in enumerate(sources[level]):
            taps = [ref[tile, pl.ds(7 + a + 2 * first, count, stride=2), :] for a in range(4)]
            down = (taps[0] + taps[3]) + 3.0 * (taps[1] + taps[2])
            high = down.astype(bf16)
            low = (down - high.astype(f32)).astype(bf16)
            for lane_at in lanes_at:
                where = pl.ds(lane_at, LANES)
                target[pl.ds(2 * place * stride + at, count), where] = high
                target[pl.ds((2 * place + 1) * stride + at, count), where] = low

    band_row = lax.broadcasted_iota(jnp.int32, (4 * LANES, LANES), 0)
    band_col = lax.broadcasted_iota(jnp.int32, (4 * LANES, LANES), 1)
    tap = band_row - (LANES - 1) - 2 * band_col
    band = jnp.where(
        jnp.logical_or(tap == 0, tap == 3),
        stencil_weights[0] / 8.0,
        jnp.where(jnp.logical_or(tap == 1, tap == 2), stencil_weights[1] / 8.0, 0.0),
    )
    right_band = jnp.where(band_col < LANES // 2, band, 0.0)[: 2 * LANES].astype(bf16)
    left_band = jnp.where(band_col >= LANES // 2, band, 0.0)[2 * LANES :].astype(bf16)
    band = band.astype(bf16)

    def across(source, count, parts):
        result = None
        for start, table in parts:
            part = jnp.dot(
                source[0 : 4 * count, pl.ds(start, table.shape[0])],
                table,
                preferred_element_type=f32,
            )
            result = part if result is None else result + part
        num = result[0:count] + result[count : 2 * count]
        den = result[2 * count : 3 * count] + result[3 * count :]
        return num / jnp.maximum(den, floor_value), den

    def own_parts(tile):
        start = tile * 2 * LANES
        if not isinstance(tile, int):
            start = pl.multiple_of(start, 2 * LANES)
        return ((start, band),)

    def side_parts(tiles_in):
        return ((tiles_in * LANES, right_band), (0, left_band))

    def tally(stat, value, cover, product):
        def parts(array):
            return array.reshape(array.shape[0] // 8, 8, LANES)

        weighted, total, largest = stat
        return (
            weighted + jnp.sum(parts(product), axis=0),
            total + jnp.sum(parts(cover), axis=0),
            jnp.maximum(largest, jnp.max(parts(value), axis=0)),
        )

    zero = jnp.zeros((8, LANES), f32)
    fresh = (zero, zero, jnp.full((8, LANES), -jnp.inf, f32))
    above_factor = jnp.where(has_above, 1.0, 0.0).astype(f32)
    below_factor = jnp.where(has_below, 1.0, 0.0).astype(f32)

    own = rows // 2
    inner = own + 2 * 8 - 2 * EDGE
    tiles_out = tiles // 2

    @pl.loop(0, tiles)
    def _(tile):
        for start in range(0, rows, 64):
            decode(tile, HALO + start, 64)
        lane_at = pl.multiple_of((tile + 1) * LANES, LANES)
        downward(0, tile, EDGE, inner, split0, 0, inner, (lane_at,))

    def inner_columns(tile, stat):
        value, cover = across(split0, inner, own_parts(tile))
        product = cover * value
        if isinstance(tile, int):
            lanes = slice(tile * LANES, (tile + 1) * LANES)
        else:
            lanes = pl.ds(pl.multiple_of(tile * LANES, LANES), LANES)
        p1[tile, 16 + EDGE : 16 + EDGE + inner, :] = product
        c1[tile, 16 + EDGE : 16 + EDGE + inner, :] = cover
        level_one[EDGE - 8 : EDGE - 8 + inner, lanes] = value
        return tally(stat, value, cover, product)

    stat = lax.fori_loop(1, tiles_out - 1, inner_columns, fresh)

    for copy in copies(0):
        copy.wait()

    @pl.when(has_below)
    def _():
        for copy in copies(1):
            copy.wait_send()
        for copy in copies(2):
            copy.wait_recv()

    @pl.when(has_above)
    def _():
        for copy in copies(2):
            copy.wait_send()
        for copy in copies(1):
            copy.wait_recv()

    sub = lax.broadcasted_iota(jnp.int32, (HALO, LANES), 0)
    for block in range(blocks):
        here = slice(block * LANES, (block + 1) * LANES)
        turn = jnp.broadcast_to(cos_rows[block : block + 1, :], (HALO, LANES))
        pieces = []
        for index, (at, shift) in enumerate(((0, 0), (LANES - HALO, 32 - HALO))):
            word = jnp.broadcast_to(side_words[index : index + 1, here], (HALO, LANES))
            flag = jnp.bitwise_and(lax.shift_right_logical(word, sub + shift), 1)
            cover = jnp.where(flag != 0, turn, 0.0)
            pieces.append((cover, cover * side[at : at + HALO, here]))
        filler = jnp.zeros((LANES - 2 * HALO, LANES), f32)
        taken, at = placed(block)
        size = taken.stop - taken.start
        for kind, ref in ((0, c0), (1, p0)):
            flat = jnp.concatenate([pieces[0][kind], filler, pieces[1][kind]], axis=0)
            ref[tiles, 8 + at : 8 + at + size, :] = jnp.transpose(flat)[taken, :]

    for tile in range(tiles):
        decode(tile, 0, HALO)
        decode(tile, HALO + rows, HALO)

    ends = (0, (tiles + 1) * LANES)
    downward(0, tiles, EDGE, inner, split0, 0, inner, ends)
    for tile in range(tiles + 1):
        lanes_at = ends if tile == tiles else ((tile + 1) * LANES,)
        downward(0, tile, 0, EDGE, edge0, 0, 2 * EDGE, lanes_at)
        downward(0, tile, EDGE + inner, EDGE, edge0, EDGE, 2 * EDGE, lanes_at)

    stats = []
    stat = inner_columns(0, stat)
    stat = inner_columns(tiles_out - 1, stat)
    value, cover = across(split0, inner, side_parts(tiles))
    p1[tiles_out, 16 + EDGE : 16 + EDGE + inner, :] = cover * value
    c1[tiles_out, 16 + EDGE : 16 + EDGE + inner, :] = cover
    for tile in range(tiles_out + 1):
        parts = side_parts(tiles) if tile == tiles_out else own_parts(tile)
        value, cover = across(edge0, 2 * EDGE, parts)
        product = cover * value
        for ref, array in ((p1, product), (c1, cover)):
            ref[tile, 16:24, :] = array[0:8] * above_factor
            ref[tile, 24 : 16 + EDGE, :] = array[8:EDGE]
            ref[tile, 16 + EDGE + inner : 24 + own, :] = array[EDGE : 2 * EDGE - 8]
            ref[tile, 24 + own : 32 + own, :] = array[2 * EDGE - 8 :] * below_factor
        if tile < tiles_out:
            lanes = slice(tile * LANES, (tile + 1) * LANES)
            level_one[0 : EDGE - 8, lanes] = value[8:EDGE]
            level_one[own - EDGE + 8 :, lanes] = value[EDGE : 2 * EDGE - 8]
            middle = slice(8, 2 * EDGE - 8)
            stat = tally(stat, value[middle], cover[middle], product[middle])
    stats.append(stat)

    splits = (None, split1, split2, split3)
    for level in range(1, LEVELS):
        source, output = splits[level], outputs[level]
        own = output.shape[0]
        last = level + 1 == LEVELS
        first = 8 if last else 0
        count = own if last else own + 16
        tiles_in = sources[level][0].shape[0] - 1
        tiles_out = output.shape[1] // LANES
        for tile in range(tiles_in + 1):
            lanes_at = (0, (tiles_in + 1) * LANES) if tile == tiles_in else ((tile + 1) * LANES,)
            downward(level, tile, first, count, source, 0, count, lanes_at)
        stat = fresh
        for tile in range(tiles_out + (not last)):
            parts = side_parts(tiles_in) if tile == tiles_out else own_parts(tile)
            value, cover = across(source, count, parts)
            product = cover * value
            middle = slice(8 - first, 8 - first + own)
            if not last:
                for ref, array in zip(sources[level + 1], (product, cover)):
                    ref[tile, 16:24, :] = array[0:8] * above_factor
                    ref[tile, 24 : 24 + own, :] = array[middle]
                    ref[tile, 24 + own : 32 + own, :] = array[8 + own :] * below_factor
            if tile < tiles_out:
                output[:, tile * LANES : (tile + 1) * LANES] = value[middle]
                stat = tally(stat, value[middle], cover[middle], product[middle])
        stats.append(stat)

    lane = lax.broadcasted_iota(jnp.int32, (8, LANES), 1)
    row = lax.broadcasted_iota(jnp.int32, (8, LANES), 0)
    mine = jnp.zeros((8, LANES), f32)
    for kind, reduce in ((0, jnp.sum), (1, jnp.sum), (2, jnp.max)):
        tile = jnp.zeros((8, LANES), f32)
        for level in range(LEVELS):
            tile = jnp.where(row == level, reduce(stats[level][kind], axis=0, keepdims=True), tile)
        mine = jnp.where(lane == row + kind * LEVELS, reduce(tile, axis=1, keepdims=True), mine)
    mine = jnp.where(row < LEVELS, mine, 0.0)
    stat_own[...] = jnp.broadcast_to(jnp.sum(mine, axis=0, keepdims=True), (8, LANES))
    sends = []
    for place, (down, right) in enumerate(others):
        copy = pltpu.make_async_remote_copy(
            src_ref=stat_own.at[0:1],
            dst_ref=stat_all.at[place : place + 1],
            send_sem=stat_send.at[place],
            recv_sem=stat_recv.at[place],
            device_id=device(down, right),
            device_id_type=MESH,
        )
        copy.start()
        sends.append(copy)
    for copy in sends:
        copy.wait()
    first = stat_own[0:1, :]
    summed = first + jnp.sum(stat_all[...], axis=0, keepdims=True)
    largest = jnp.maximum(first, jnp.max(stat_all[...], axis=0, keepdims=True))
    summed = jnp.broadcast_to(summed, (8, LANES))
    largest = jnp.broadcast_to(largest, (8, LANES))

    def pick(array, kind):
        here = jnp.logical_and(lane == row + kind * LEVELS, row < LEVELS)
        return jnp.sum(jnp.where(here, array, 0.0), axis=1, keepdims=True)

    level_means = pick(summed, 0) / (pick(summed, 1) + mean_eps)
    diagonal = jnp.logical_and(lane == row, row < LEVELS)
    means_ref[...] = jnp.sum(jnp.where(diagonal, level_means, 0.0), axis=0)[0:LEVELS]
    maxima_ref[...] = jnp.sum(jnp.where(diagonal, pick(largest, 2), 0.0), axis=0)[0:LEVELS]


def per_device(row_devices, col_devices, surface_field, land_words):
    rows, cols = surface_field.shape
    tiles = cols // LANES
    levels = tuple(
        jax.ShapeDtypeStruct((rows >> level, cols >> level), f32) for level in range(1, LEVELS + 1)
    )
    blocks = rows // LANES + 2
    scratch = [
        pltpu.VMEM((tiles, rows + 2 * HALO, LANES), f32),
        pltpu.VMEM((land_words.shape[1], rows), jnp.int32),
        pltpu.VMEM((rows + 2 * HALO, LANES), jnp.int32),
        pltpu.VMEM((rows + 2 * HALO, LANES), f32),
        pltpu.VMEM((8 * (-(-blocks // 8)), LANES), f32),
        pltpu.VMEM((HALO, rows), f32),
        pltpu.VMEM((HALO, rows), f32),
        pltpu.VMEM((LANES, rows + 2 * LANES), f32),
        pltpu.VMEM((8, rows + 2 * LANES), jnp.int32),
    ]
    for level in range(LEVELS):
        shape = ((cols >> level) // LANES + 1, (rows >> level) + 48, LANES)
        scratch += [pltpu.VMEM(shape, f32)] * 2
    scratch += [
        pltpu.VMEM((4 * (rows // 2 + 16 - 2 * EDGE), cols + 2 * LANES), bf16),
        pltpu.VMEM((8 * EDGE, cols + 2 * LANES), bf16),
    ]
    for level in range(1, LEVELS):
        margin = 16 if level + 1 < LEVELS else 0
        shape = (4 * ((rows >> (level + 1)) + margin), (cols >> level) + 2 * LANES)
        scratch.append(pltpu.VMEM(shape, bf16))
    others = row_devices * col_devices - 1
    scratch += [
        pltpu.VMEM((8, LANES), f32),
        pltpu.VMEM((others, LANES), f32),
        pltpu.SemaphoreType.DMA((tiles,)),
        pltpu.SemaphoreType.DMA,
        pltpu.SemaphoreType.DMA((16,)),
        pltpu.SemaphoreType.DMA((16,)),
        pltpu.SemaphoreType.DMA((others,)),
        pltpu.SemaphoreType.DMA((others,)),
    ]
    vmem = pl.BlockSpec(memory_space=pltpu.VMEM)
    small = jax.ShapeDtypeStruct((LEVELS,), f32)
    results = (*levels, small, small)
    found = pl.pallas_call(
        functools.partial(kernel, row_devices, col_devices),
        out_shape=tuple(pltpu.VMEM(each.shape, each.dtype) for each in results),
        in_specs=[pl.BlockSpec(memory_space=pltpu.HBM)] * 2,
        out_specs=(vmem,) * len(results),
        scratch_shapes=scratch,
        compiler_params=pltpu.CompilerParams(
            collective_id=0, has_side_effects=True, vmem_limit_bytes=56 * 1024 * 1024
        ),
        name="coarsen_levels",
    )(surface_field, land_words.T)

    return pl.pallas_call(
        hand_over,
        out_shape=results,
        in_specs=[vmem] * len(results),
        out_specs=(pl.BlockSpec(memory_space=pl.ANY),) * len(results),
        scratch_shapes=[pltpu.SemaphoreType.DMA((len(results),))],
        compiler_params=pltpu.CompilerParams(vmem_limit_bytes=8 * 1024 * 1024),
        name="hand_over",
    )(*found)


def hand_over(*refs):
    count = LEVELS + 2
    sources, targets, sems = refs[:count], refs[count : 2 * count], refs[2 * count]
    copies = [
        pltpu.make_async_copy(sources[at], targets[at], sems.at[at]) for at in range(count)
    ]
    for copy in copies:
        copy.start()
    for copy in copies:
        copy.wait()


def solution(mesh):
    return jax.shard_map(
        functools.partial(per_device, mesh.shape["rows"], mesh.shape["cols"]),
        mesh=mesh,
        in_specs=(P("rows", "cols"), P("rows", "cols")),
        out_specs=(P("rows", "cols"),) * LEVELS + (P(), P()),
        check_vma=False,
    )
```

time: 31.4 us -> 24.3 us (0.77)
  Pallas kernels: 30.6 us -> 23.5 us
    pallas_call x1, Pallas kernels: 29.5 us -> 22.4 us  [per_device(): pl.pallas_call(functools.partial(kernel, row_devices, col_devices), out_s...]
where the time goes in v2:
time: 24.3 us; the launch traced here: 24.1 us
  Pallas kernels  23.5 us (97%)
  between operations  0.64 us (3%)
    pallas_call x1, Pallas kernels, per_device(): pl.pallas_call(functools.partial(kernel, row_devices, col_devices), out_s...  22.4 us
    pallas_call x1, Pallas kernels, per_device(): pl.pallas_call(hand_over, out_shape=results, in_specs=[vmem] * len(result...  1.12 us

profile of v2, /device:TPU:0, one launch (start us, length us, event | category | flops | bytes accessed | tf_op | source)
XLA Modules:
  0.0 24.1 jit_solution(7778955833719645392)
XLA Ops:
  0.6 22.4 %coarsen_levels.1 = (f32[256,1024]{1,0:T(8,128)S(1)}, f32[128,512]{1,0:T(8,128)S(1)}, f32[64,256]{1,0:T(8,128)S(1)}, f32[32,128]{1,0:T(8,128)S(1)}, f32[4]{0:T(128)S(1)}, /*index=5*/f32[4]{0:T(128)S(1)}) custom-call(f32[512,2048]{1,0:T(8,128)} %field.1, s32[64,512]{1,0:T(8,128)} %bitcast.1), custom_call_target="tpu_custom_call" | custom-call | tf_op jit(solution)/shard_map/coarsen_levels/pallas_call | solution.py:513
  23.0 1.1 %hand_over.1 = (f32[256,1024]{1,0:T(8,128)}, f32[128,512]{1,0:T(8,128)}, f32[64,256]{1,0:T(8,128)}, f32[32,128]{1,0:T(8,128)}, f32[4]{0:T(128)}, /*index=5*/f32[4]{0:T(128)}) custom-call(f32[256,1024]{1,0:T(8,128)S(1)} %get-tuple-element.12.refs_0_, f32[128,512]{1,0:T(8,128)S(1)} %get-tuple-element.13.refs_1_, f32[64,256]{1,0:T(8,128)S(1)} %get-tuple-element.14.refs_2_, ...), custom_call_target="tpu_custom_call" | custom-call | tf_op jit(solution)/shard_map/hand_over/pallas_call | solution.py:525

commit v3 on v2

--- a/solution.py
+++ b/solution.py
@@ -49,10 +49,17 @@
     p3,
     c3,
     split0,
-    edge0,
     split1,
     split2,
     split3,
+    edge0,
+    edge1,
+    edge2,
+    edge3,
+    partial0,
+    partial1,
+    partial2,
+    partial3,
     stat_own,
     stat_all,
     load_sem,
@@ -98,8 +105,11 @@
         return pltpu.make_async_copy(
             field.at[:, pl.ds(start, LANES)],
             fine.at[tile, pl.ds(HALO, rows), :],
-            load_sem.at[tile],
-        )
+            load_sem.at[0 if tile == 0 else 2 if tile < tiles - 1 else 1],
+        )
+
+    def settle(ref, sem):
+        pltpu.make_async_copy(ref, ref, sem).wait()
 
     order = [0, tiles - 1, *range(1, tiles - 1)]
     for tile in order:
@@ -132,8 +142,7 @@
     send_left[...] = jnp.transpose(fine[0, HALO : HALO + rows, :])[0:HALO, :]
     load(tiles - 1).wait()
     send_right[...] = jnp.transpose(fine[tiles - 1, HALO : HALO + rows, :])[LANES - HALO :, :]
-    for tile in range(1, tiles - 1):
-        load(tile).wait()
+    settle(fine.at[1 : tiles - 1, HALO : HALO + rows, :], load_sem.at[2])
 
     pl.semaphore_wait(barrier, len(others))
 
@@ -159,6 +168,8 @@
         (words.at[rows : rows + HALO, :], words.at[0:HALO, :], (1, 0)),
         (send_left.at[:, behind], right_side.at[:, top_lanes], (1, -1)),
         (send_right.at[:, behind], left_side.at[:, top_lanes], (1, 1)),
+    )
+    down_words_plan = (
         (first_words.at[:, behind], right_words.at[:, top_lanes], (1, -1)),
         (last_words.at[:, behind], left_words.at[:, top_lanes], (1, 1)),
     )
@@ -167,23 +178,32 @@
         (words.at[HALO : 2 * HALO, :], words.at[HALO + rows :, :], (-1, 0)),
         (send_left.at[:, ahead], right_side.at[:, bottom_lanes], (-1, -1)),
         (send_right.at[:, ahead], left_side.at[:, bottom_lanes], (-1, 1)),
+    )
+    up_words_plan = (
         (first_words.at[:, ahead], right_words.at[:, bottom_lanes], (-1, -1)),
         (last_words.at[:, ahead], left_words.at[:, bottom_lanes], (-1, 1)),
     )
-    plans = (across_plan, down_plan, up_plan)
-    first_slot = (0, len(across_plan), len(across_plan) + len(down_plan))
+    plans = (across_plan, down_plan, up_plan, down_words_plan, up_words_plan)
+    downs, ups = (1, 3), (2, 4)
+
+    def settle_halo(which, sem):
+        moved = sum(math.prod(source.shape) for source, _, _ in plans[which])
+        if moved % (8 * LANES):
+            settle(side_words.at[0:1, 0:moved], sem.at[which])
+        else:
+            settle(fine.at[0, 0 : moved // LANES, :], sem.at[which])
 
     def copies(which):
         return [
             pltpu.make_async_remote_copy(
                 src_ref=source,
                 dst_ref=target,
-                send_sem=halo_send.at[first_slot[which] + place],
-                recv_sem=halo_recv.at[first_slot[which] + place],
+                send_sem=halo_send.at[which],
+                recv_sem=halo_recv.at[which],
                 device_id=device(down, right),
                 device_id_type=MESH,
             )
-            for place, (source, target, (down, right)) in enumerate(plans[which])
+            for source, target, (down, right) in plans[which]
         ]
 
     for copy in copies(0):
@@ -191,13 +211,15 @@
 
     @pl.when(has_below)
     def _():
-        for copy in copies(1):
-            copy.start()
+        for which in downs:
+            for copy in copies(which):
+                copy.start()
 
     @pl.when(has_above)
     def _():
-        for copy in copies(2):
-            copy.start()
+        for which in ups:
+            for copy in copies(which):
+                copy.start()
 
     blocks = rows // LANES + 2
     packed = cos_rows.shape
@@ -243,52 +265,84 @@
         p0[tile, pl.ds(8 + start, count), :] = cover * fine[tile, pl.ds(start, count), :]
 
     sources = ((p0, c0), (p1, c1), (p2, c2), (p3, c3))
+    splits = (split0, split1, split2, split3)
+    edges = (edge0, edge1, edge2, edge3)
+    partials = (partial0, partial1, partial2, partial3)
     outputs = (level_one, level_two, level_three, level_four)
 
-    def downward(level, tile, first, count, target, at, stride, lanes_at):
+    def downward(level, tile, first, count, target, at, stride):
+        lanes = pl.ds(tile * LANES, LANES)
         for place, ref in enumerate(sources[level]):
             taps = [ref[tile, pl.ds(7 + a + 2 * first, count, stride=2), :] for a in range(4)]
             down = (taps[0] + taps[3]) + 3.0 * (taps[1] + taps[2])
             high = down.astype(bf16)
             low = (down - high.astype(f32)).astype(bf16)
-            for lane_at in lanes_at:
-                where = pl.ds(lane_at, LANES)
-                target[pl.ds(2 * place * stride + at, count), where] = high
-                target[pl.ds((2 * place + 1) * stride + at, count), where] = low
+            target[pl.ds(2 * place * stride + at, count), lanes] = high
+            target[pl.ds((2 * place + 1) * stride + at, count), lanes] = low
+
+    def table(tap, keep=True):
+        weight = jnp.where(
+            jnp.logical_or(tap == 0, tap == 3),
+            stencil_weights[0] / 8.0,
+            jnp.where(jnp.logical_or(tap == 1, tap == 2), stencil_weights[1] / 8.0, 0.0),
+        )
+        return jnp.where(keep, weight, 0.0).astype(bf16)
 
     band_row = lax.broadcasted_iota(jnp.int32, (4 * LANES, LANES), 0)
     band_col = lax.broadcasted_iota(jnp.int32, (4 * LANES, LANES), 1)
-    tap = band_row - (LANES - 1) - 2 * band_col
-    band = jnp.where(
-        jnp.logical_or(tap == 0, tap == 3),
-        stencil_weights[0] / 8.0,
-        jnp.where(jnp.logical_or(tap == 1, tap == 2), stencil_weights[1] / 8.0, 0.0),
-    )
-    right_band = jnp.where(band_col < LANES // 2, band, 0.0)[: 2 * LANES].astype(bf16)
-    left_band = jnp.where(band_col >= LANES // 2, band, 0.0)[2 * LANES :].astype(bf16)
-    band = band.astype(bf16)
+    band = table(band_row - (LANES - 1) - 2 * band_col)
+
+    half = LANES // 2
+
+    def column(at):
+        middle = jnp.where(at == half, 0, -1)
+        away = jnp.where(at > half, at - LANES, at)
+        return jnp.where(jnp.logical_or(at == half, at == half - 1), middle, away)
+
+    lane_in = lax.broadcasted_iota(jnp.int32, (LANES, LANES), 0)
+    lane_out = lax.broadcasted_iota(jnp.int32, (LANES, LANES), 1)
+    leftward = lane_out >= half
+    from_side = table(
+        column(lane_in) - 2 * column(lane_out) + 1, (lane_in >= half) == leftward
+    )
+    from_first = table(lane_in - 2 * column(lane_out) + 1, leftward)
+    from_last = table(lane_in - LANES - 2 * column(lane_out) + 1, jnp.logical_not(leftward))
+    last_and_side = jnp.concatenate([from_last, from_side], axis=0)
 
     def across(source, count, parts):
         result = None
-        for start, table in parts:
+        for start, weights in parts:
             part = jnp.dot(
-                source[0 : 4 * count, pl.ds(start, table.shape[0])],
-                table,
+                source[0 : 4 * count, start * LANES : start * LANES + weights.shape[0]],
+                weights,
                 preferred_element_type=f32,
             )
             result = part if result is None else result + part
         num = result[0:count] + result[count : 2 * count]
         den = result[2 * count : 3 * count] + result[3 * count :]
-        return num / jnp.maximum(den, floor_value), den
-
-    def own_parts(tile):
-        start = tile * 2 * LANES
-        if not isinstance(tile, int):
-            start = pl.multiple_of(start, 2 * LANES)
-        return ((start, band),)
-
-    def side_parts(tiles_in):
-        return ((tiles_in * LANES, right_band), (0, left_band))
+        return num, den
+
+    def own_parts(tile, tiles_in):
+        start = max(2 * tile - 1, 0)
+        stop = min(2 * tile + 3, tiles_in)
+        skip = start - (2 * tile - 1)
+        return ((start, band[skip * LANES : (skip + stop - start) * LANES]),)
+
+    def finish(num, den):
+        value = num / jnp.maximum(den, floor_value)
+        return value, den, den * value
+
+    def ring(shape, tile, count_tiles):
+        lanes = lax.broadcasted_iota(jnp.int32, shape, 1)
+        if tile == count_tiles:
+            return jnp.logical_or(lanes == half, lanes == half - 1)
+        here = None
+        if tile == 0:
+            here = lanes == 0
+        if tile == count_tiles - 1:
+            final = lanes == LANES - 1
+            here = final if here is None else jnp.logical_or(here, final)
+        return here
 
     def tally(stat, value, cover, product):
         def parts(array):
@@ -301,52 +355,72 @@
             jnp.maximum(largest, jnp.max(parts(value), axis=0)),
         )
 
+    def masked(level, tile, value, cover, product):
+        count_tiles = outputs[level].shape[1] // LANES
+        here = ring(value.shape, tile, count_tiles)
+        if tile == count_tiles:
+            inside = jnp.where(here, value, -jnp.inf)
+            return cover, product, (inside, jnp.where(here, cover, 0.0), jnp.where(here, product, 0.0))
+        if here is not None:
+            value = jnp.where(here, -jnp.inf, value)
+            cover = jnp.where(here, 0.0, cover)
+            product = jnp.where(here, 0.0, product)
+        return cover, product, (value, cover, product)
+
     zero = jnp.zeros((8, LANES), f32)
-    fresh = (zero, zero, jnp.full((8, LANES), -jnp.inf, f32))
+    stats = [(zero, zero, jnp.full((8, LANES), -jnp.inf, f32)) for _ in range(LEVELS)]
     above_factor = jnp.where(has_above, 1.0, 0.0).astype(f32)
     below_factor = jnp.where(has_below, 1.0, 0.0).astype(f32)
 
-    own = rows // 2
-    inner = own + 2 * 8 - 2 * EDGE
-    tiles_out = tiles // 2
-
-    @pl.loop(0, tiles)
-    def _(tile):
-        for start in range(0, rows, 64):
-            decode(tile, HALO + start, 64)
-        lane_at = pl.multiple_of((tile + 1) * LANES, LANES)
-        downward(0, tile, EDGE, inner, split0, 0, inner, (lane_at,))
-
-    def inner_columns(tile, stat):
-        value, cover = across(split0, inner, own_parts(tile))
-        product = cover * value
-        if isinstance(tile, int):
+    def inner_rows(level):
+        return outputs[level].shape[0] + 16 - 2 * EDGE
+
+    def inner_tile(level, tile, num, den):
+        inner = inner_rows(level)
+        value, cover, product = finish(num, den)
+        cover, product, counted = masked(level, tile, value, cover, product)
+        if level + 1 < LEVELS:
+            for ref, array in zip(sources[level + 1], (product, cover)):
+                ref[tile, 16 + EDGE : 16 + EDGE + inner, :] = array
+        stats[level] = tally(stats[level], *counted)
+        return value
+
+    for level in range(LEVELS):
+        inner = inner_rows(level)
+        tiles_in = sources[level][0].shape[0] - 1
+        tiles_out = outputs[level].shape[1] // LANES
+
+        def feed(tile):
+            if level == 0:
+                for start in range(0, rows, 64):
+                    decode(tile, HALO + start, 64)
+            downward(level, tile, EDGE, inner, splits[level], 0, inner)
+
+        fed = 0
+        for tile in range(tiles_out):
+            while fed < min(2 * tile + 3, tiles_in):
+                feed(fed)
+                fed += 1
+            value = inner_tile(
+                level, tile, *across(splits[level], inner, own_parts(tile, tiles_in))
+            )
             lanes = slice(tile * LANES, (tile + 1) * LANES)
-        else:
-            lanes = pl.ds(pl.multiple_of(tile * LANES, LANES), LANES)
-        p1[tile, 16 + EDGE : 16 + EDGE + inner, :] = product
-        c1[tile, 16 + EDGE : 16 + EDGE + inner, :] = cover
-        level_one[EDGE - 8 : EDGE - 8 + inner, lanes] = value
-        return tally(stat, value, cover, product)
-
-    stat = lax.fori_loop(1, tiles_out - 1, inner_columns, fresh)
-
-    for copy in copies(0):
-        copy.wait()
+            outputs[level][EDGE - 8 : EDGE - 8 + inner, lanes] = value
+        num, den = across(splits[level], inner, ((0, from_first), (tiles_in - 1, from_last)))
+        partials[level][0] = num
+        partials[level][1] = den
+
+    settle_halo(0, halo_recv)
 
     @pl.when(has_below)
     def _():
-        for copy in copies(1):
-            copy.wait_send()
-        for copy in copies(2):
-            copy.wait_recv()
+        for which in ups:
+            settle_halo(which, halo_recv)
 
     @pl.when(has_above)
     def _():
-        for copy in copies(2):
-            copy.wait_send()
-        for copy in copies(1):
-            copy.wait_recv()
+        for which in downs:
+            settle_halo(which, halo_recv)
 
     sub = lax.broadcasted_iota(jnp.int32, (HALO, LANES), 0)
     for block in range(blocks):
@@ -369,102 +443,106 @@
         decode(tile, 0, HALO)
         decode(tile, HALO + rows, HALO)
 
-    ends = (0, (tiles + 1) * LANES)
-    downward(0, tiles, EDGE, inner, split0, 0, inner, ends)
-    for tile in range(tiles + 1):
-        lanes_at = ends if tile == tiles else ((tile + 1) * LANES,)
-        downward(0, tile, 0, EDGE, edge0, 0, 2 * EDGE, lanes_at)
-        downward(0, tile, EDGE + inner, EDGE, edge0, EDGE, 2 * EDGE, lanes_at)
-
-    stats = []
-    stat = inner_columns(0, stat)
-    stat = inner_columns(tiles_out - 1, stat)
-    value, cover = across(split0, inner, side_parts(tiles))
-    p1[tiles_out, 16 + EDGE : 16 + EDGE + inner, :] = cover * value
-    c1[tiles_out, 16 + EDGE : 16 + EDGE + inner, :] = cover
-    for tile in range(tiles_out + 1):
-        parts = side_parts(tiles) if tile == tiles_out else own_parts(tile)
-        value, cover = across(edge0, 2 * EDGE, parts)
-        product = cover * value
-        for ref, array in ((p1, product), (c1, cover)):
-            ref[tile, 16:24, :] = array[0:8] * above_factor
-            ref[tile, 24 : 16 + EDGE, :] = array[8:EDGE]
-            ref[tile, 16 + EDGE + inner : 24 + own, :] = array[EDGE : 2 * EDGE - 8]
-            ref[tile, 24 + own : 32 + own, :] = array[2 * EDGE - 8 :] * below_factor
-        if tile < tiles_out:
-            lanes = slice(tile * LANES, (tile + 1) * LANES)
-            level_one[0 : EDGE - 8, lanes] = value[8:EDGE]
-            level_one[own - EDGE + 8 :, lanes] = value[EDGE : 2 * EDGE - 8]
-            middle = slice(8, 2 * EDGE - 8)
-            stat = tally(stat, value[middle], cover[middle], product[middle])
-    stats.append(stat)
-
-    splits = (None, split1, split2, split3)
-    for level in range(1, LEVELS):
-        source, output = splits[level], outputs[level]
+    ring_values = []
+    for level in range(LEVELS):
+        inner = inner_rows(level)
+        output = outputs[level]
         own = output.shape[0]
-        last = level + 1 == LEVELS
-        first = 8 if last else 0
-        count = own if last else own + 16
         tiles_in = sources[level][0].shape[0] - 1
         tiles_out = output.shape[1] // LANES
+        downward(level, tiles_in, EDGE, inner, splits[level], 0, inner)
         for tile in range(tiles_in + 1):
-            lanes_at = (0, (tiles_in + 1) * LANES) if tile == tiles_in else ((tile + 1) * LANES,)
-            downward(level, tile, first, count, source, 0, count, lanes_at)
-        stat = fresh
-        for tile in range(tiles_out + (not last)):
-            parts = side_parts(tiles_in) if tile == tiles_out else own_parts(tile)
-            value, cover = across(source, count, parts)
-            product = cover * value
-            middle = slice(8 - first, 8 - first + own)
-            if not last:
+            downward(level, tile, 0, EDGE, edges[level], 0, 2 * EDGE)
+            downward(level, tile, EDGE + inner, EDGE, edges[level], EDGE, 2 * EDGE)
+        num, den = across(splits[level], inner, ((tiles_in, from_side),))
+        inner_value = inner_tile(
+            level, tiles_out, num + partials[level][0], den + partials[level][1]
+        )
+        for tile in range(tiles_out + 1):
+            if tile == tiles_out:
+                parts = ((tiles_in - 1, last_and_side), (0, from_first))
+            else:
+                parts = own_parts(tile, tiles_in)
+            value, cover, product = finish(*across(edges[level], 2 * EDGE, parts))
+            cover, product, counted = masked(level, tile, value, cover, product)
+            if level + 1 < LEVELS:
                 for ref, array in zip(sources[level + 1], (product, cover)):
                     ref[tile, 16:24, :] = array[0:8] * above_factor
-                    ref[tile, 24 : 24 + own, :] = array[middle]
-                    ref[tile, 24 + own : 32 + own, :] = array[8 + own :] * below_factor
+                    ref[tile, 24 : 16 + EDGE, :] = array[8:EDGE]
+                    ref[tile, 16 + EDGE + inner : 24 + own, :] = array[EDGE : 2 * EDGE - 8]
+                    ref[tile, 24 + own : 32 + own, :] = array[2 * EDGE - 8 :] * below_factor
+            middle = slice(8, 2 * EDGE - 8)
+            stats[level] = tally(stats[level], *(array[middle] for array in counted))
             if tile < tiles_out:
-                output[:, tile * LANES : (tile + 1) * LANES] = value[middle]
-                stat = tally(stat, value[middle], cover[middle], product[middle])
-        stats.append(stat)
+                lanes = slice(tile * LANES, (tile + 1) * LANES)
+                output[0 : EDGE - 8, lanes] = value[8:EDGE]
+                output[own - EDGE + 8 :, lanes] = value[EDGE : 2 * EDGE - 8]
+            else:
+                ring_values.append((inner_value, value[middle]))
 
     lane = lax.broadcasted_iota(jnp.int32, (8, LANES), 1)
     row = lax.broadcasted_iota(jnp.int32, (8, LANES), 0)
-    mine = jnp.zeros((8, LANES), f32)
-    for kind, reduce in ((0, jnp.sum), (1, jnp.sum), (2, jnp.max)):
-        tile = jnp.zeros((8, LANES), f32)
-        for level in range(LEVELS):
-            tile = jnp.where(row == level, reduce(stats[level][kind], axis=0, keepdims=True), tile)
-        mine = jnp.where(lane == row + kind * LEVELS, reduce(tile, axis=1, keepdims=True), mine)
-    mine = jnp.where(row < LEVELS, mine, 0.0)
-    stat_own[...] = jnp.broadcast_to(jnp.sum(mine, axis=0, keepdims=True), (8, LANES))
-    sends = []
+    mine = zero
+    for level, (weighted, total, largest) in enumerate(stats):
+        weighted = jnp.sum(weighted, axis=0, keepdims=True)
+        total = jnp.sum(total, axis=0, keepdims=True)
+        sums = jnp.sum(jnp.where(row == 0, weighted, total), axis=1, keepdims=True)
+        largest = jnp.max(largest, axis=0, keepdims=True)
+        largest = jnp.max(jnp.broadcast_to(largest, (8, LANES)), axis=1, keepdims=True)
+        mine = jnp.where(lane == level, jnp.where(row < 2, sums, largest), mine)
+    stat_own[...] = mine
     for place, (down, right) in enumerate(others):
         copy = pltpu.make_async_remote_copy(
-            src_ref=stat_own.at[0:1],
-            dst_ref=stat_all.at[place : place + 1],
-            send_sem=stat_send.at[place],
-            recv_sem=stat_recv.at[place],
+            src_ref=stat_own.at[0:4],
+            dst_ref=stat_all.at[place, 0:4],
+            send_sem=stat_send,
+            recv_sem=stat_recv,
             device_id=device(down, right),
             device_id_type=MESH,
         )
         copy.start()
-        sends.append(copy)
-    for copy in sends:
-        copy.wait()
-    first = stat_own[0:1, :]
-    summed = first + jnp.sum(stat_all[...], axis=0, keepdims=True)
-    largest = jnp.maximum(first, jnp.max(stat_all[...], axis=0, keepdims=True))
-    summed = jnp.broadcast_to(summed, (8, LANES))
-    largest = jnp.broadcast_to(largest, (8, LANES))
-
-    def pick(array, kind):
-        here = jnp.logical_and(lane == row + kind * LEVELS, row < LEVELS)
-        return jnp.sum(jnp.where(here, array, 0.0), axis=1, keepdims=True)
-
-    level_means = pick(summed, 0) / (pick(summed, 1) + mean_eps)
-    diagonal = jnp.logical_and(lane == row, row < LEVELS)
-    means_ref[...] = jnp.sum(jnp.where(diagonal, level_means, 0.0), axis=0)[0:LEVELS]
-    maxima_ref[...] = jnp.sum(jnp.where(diagonal, pick(largest, 2), 0.0), axis=0)[0:LEVELS]
+
+    for output, (inner_value, edge_value) in zip(outputs, ring_values):
+        own, width = output.shape
+        tiles_out = width // LANES
+        for start, array in (
+            (0, edge_value[0:8]),
+            (8, inner_value),
+            (own - 8, edge_value[8:16]),
+        ):
+            turned = pltpu.roll(array, half, axis=1)
+            here = slice(start, start + array.shape[0])
+            for tile in sorted({0, tiles_out - 1}):
+                lanes = slice(tile * LANES, (tile + 1) * LANES)
+                at_ring = ring(array.shape, tile, tiles_out)
+                output[here, lanes] = jnp.where(at_ring, turned, output[here, lanes])
+
+    settle_halo(0, halo_send)
+
+    @pl.when(has_below)
+    def _():
+        for which in downs:
+            settle_halo(which, halo_send)
+
+    @pl.when(has_above)
+    def _():
+        for which in ups:
+            settle_halo(which, halo_send)
+
+    arrived = stat_all.at[:, 0:4, :]
+    settle(arrived, stat_recv)
+
+    def combine(reduce):
+        parts = [stat_own[0:4, :]] + [stat_all[place, 0:4, :] for place in range(len(others))]
+        while len(parts) > 1:
+            pairs = [reduce(*pair) for pair in zip(parts[0::2], parts[1::2])]
+            parts = pairs + parts[2 * len(pairs) :]
+        return parts[0]
+
+    summed, largest = combine(jnp.add), combine(jnp.maximum)
+    means_ref[...] = jnp.sum(summed[0:1] / (summed[1:2] + mean_eps), axis=0)[0:LEVELS]
+    maxima_ref[...] = jnp.sum(largest[2:3], axis=0)[0:LEVELS]
+    settle(arrived, stat_send)
 
 
 def per_device(row_devices, col_devices, surface_field, land_words):
@@ -488,24 +566,24 @@
     for level in range(LEVELS):
         shape = ((cols >> level) // LANES + 1, (rows >> level) + 48, LANES)
         scratch += [pltpu.VMEM(shape, f32)] * 2
-    scratch += [
-        pltpu.VMEM((4 * (rows // 2 + 16 - 2 * EDGE), cols + 2 * LANES), bf16),
-        pltpu.VMEM((8 * EDGE, cols + 2 * LANES), bf16),
-    ]
-    for level in range(1, LEVELS):
-        margin = 16 if level + 1 < LEVELS else 0
-        shape = (4 * ((rows >> (level + 1)) + margin), (cols >> level) + 2 * LANES)
-        scratch.append(pltpu.VMEM(shape, bf16))
+    for level in range(LEVELS):
+        inner = (rows >> (level + 1)) + 16 - 2 * EDGE
+        scratch.append(pltpu.VMEM((4 * inner, (cols >> level) + LANES), bf16))
+    for level in range(LEVELS):
+        scratch.append(pltpu.VMEM((8 * EDGE, (cols >> level) + LANES), bf16))
+    for level in range(LEVELS):
+        inner = (rows >> (level + 1)) + 16 - 2 * EDGE
+        scratch.append(pltpu.VMEM((2, inner, LANES), f32))
     others = row_devices * col_devices - 1
     scratch += [
         pltpu.VMEM((8, LANES), f32),
-        pltpu.VMEM((others, LANES), f32),
-        pltpu.SemaphoreType.DMA((tiles,)),
+        pltpu.VMEM((others, 8, LANES), f32),
+        pltpu.SemaphoreType.DMA((3,)),
         pltpu.SemaphoreType.DMA,
-        pltpu.SemaphoreType.DMA((16,)),
-        pltpu.SemaphoreType.DMA((16,)),
-        pltpu.SemaphoreType.DMA((others,)),
-        pltpu.SemaphoreType.DMA((others,)),
+        pltpu.SemaphoreType.DMA((5,)),
+        pltpu.SemaphoreType.DMA((5,)),
+        pltpu.SemaphoreType.DMA,
+        pltpu.SemaphoreType.DMA,
     ]
     vmem = pl.BlockSpec(memory_space=pltpu.VMEM)
     small = jax.ShapeDtypeStruct((LEVELS,), f32)

time: 24.3 us -> 20.2 us (0.83)
  Pallas kernels: 23.5 us -> 19.4 us
    pallas_call x1, Pallas kernels: 22.4 us -> 18.3 us  [per_device(): pl.pallas_call(functools.partial(kernel, row_devices, col_devices), out_s...]
where the time goes in v3:
time: 20.2 us; the launch traced here: 20 us
  Pallas kernels  19.4 us (96%)
  between operations  0.64 us (3%)
    pallas_call x1, Pallas kernels, per_device(): pl.pallas_call(functools.partial(kernel, row_devices, col_devices), out_s...  18.3 us
    pallas_call x1, Pallas kernels, per_device(): pl.pallas_call(hand_over, out_shape=results, in_specs=[vmem] * len(result...  1.12 us

profile of v3, /device:TPU:0, one launch (start us, length us, event | category | flops | bytes accessed | tf_op | source)
XLA Modules:
  0.0 20.0 jit_solution(12750430936536412937)
XLA Ops:
  0.6 18.3 %coarsen_levels.1 = (f32[256,1024]{1,0:T(8,128)S(1)}, f32[128,512]{1,0:T(8,128)S(1)}, f32[64,256]{1,0:T(8,128)S(1)}, f32[32,128]{1,0:T(8,128)S(1)}, f32[4]{0:T(128)S(1)}, /*index=5*/f32[4]{0:T(128)S(1)}) custom-call(f32[512,2048]{1,0:T(8,128)} %field.1, s32[64,512]{1,0:T(8,128)} %bitcast.1), custom_call_target="tpu_custom_call" | custom-call | tf_op jit(solution)/shard_map/coarsen_levels/pallas_call | solution.py:591
  18.9 1.1 %hand_over.1 = (f32[256,1024]{1,0:T(8,128)}, f32[128,512]{1,0:T(8,128)}, f32[64,256]{1,0:T(8,128)}, f32[32,128]{1,0:T(8,128)}, f32[4]{0:T(128)}, /*index=5*/f32[4]{0:T(128)}) custom-call(f32[256,1024]{1,0:T(8,128)S(1)} %get-tuple-element.12.refs_0_, f32[128,512]{1,0:T(8,128)S(1)} %get-tuple-element.13.refs_1_, f32[64,256]{1,0:T(8,128)S(1)} %get-tuple-element.14.refs_2_, ...), custom_call_target="tpu_custom_call" | custom-call | tf_op jit(solution)/shard_map/hand_over/pallas_call | solution.py:603

commit v4 on v3

--- a/solution.py
+++ b/solution.py
@@ -15,6 +15,7 @@
 LANES = 128
 HALO = 16
 EDGE = 16
+CHUNK = 80
 MESH = pl.DeviceIdType.MESH
 f32 = jnp.float32
 bf16 = jnp.bfloat16
@@ -52,10 +53,6 @@
     split1,
     split2,
     split3,
-    edge0,
-    edge1,
-    edge2,
-    edge3,
     partial0,
     partial1,
     partial2,
@@ -68,6 +65,7 @@
     halo_recv,
     stat_send,
     stat_recv,
+    column_sem,
 ):
     rows, cols = field.shape
     tiles = cols // LANES
@@ -91,17 +89,17 @@
         if (down, right) != (0, 0)
     ]
 
-    barrier = pltpu.get_barrier_semaphore()
-    for down, right in others:
-        pl.semaphore_signal(barrier, inc=1, device_id=device(down, right), device_id_type=MESH)
-
+    near = [
+        (down, right)
+        for down, right in others
+        if down == 0
+        or right == 0
+        or (down in (1, row_devices - 1) and right in (1, col_devices - 1))
+    ]
     land_load = pltpu.make_async_copy(land_words, land, land_sem)
-    land_load.start()
 
     def load(tile):
         start = tile * LANES
-        if not isinstance(tile, int):
-            start = pl.multiple_of(start, LANES)
         return pltpu.make_async_copy(
             field.at[:, pl.ds(start, LANES)],
             fine.at[tile, pl.ds(HALO, rows), :],
@@ -111,8 +109,15 @@
     def settle(ref, sem):
         pltpu.make_async_copy(ref, ref, sem).wait()
 
-    order = [0, tiles - 1, *range(1, tiles - 1)]
-    for tile in order:
+    load(0).start()
+    load(tiles - 1).start()
+    land_load.start()
+
+    barrier = pltpu.get_barrier_semaphore()
+    for down, right in near:
+        pl.semaphore_signal(barrier, inc=1, device_id=device(down, right), device_id_type=MESH)
+
+    for tile in range(1, tiles - 1):
         load(tile).start()
 
     def clear(row_start, lane_start):
@@ -131,20 +136,17 @@
     def _():
         clear(HALO + rows, LANES + rows)
 
+    load(0).wait()
+    load(tiles - 1).wait()
     land_load.wait()
-    upright = land[...]
-    if count_words < LANES:
-        filler = jnp.zeros((LANES - count_words, rows), jnp.int32)
-        upright = jnp.concatenate([upright, filler], axis=0)
-    words[HALO : HALO + rows, :] = jnp.transpose(upright)
-
-    load(0).wait()
-    send_left[...] = jnp.transpose(fine[0, HALO : HALO + rows, :])[0:HALO, :]
-    load(tiles - 1).wait()
-    send_right[...] = jnp.transpose(fine[tiles - 1, HALO : HALO + rows, :])[LANES - HALO :, :]
-    settle(fine.at[1 : tiles - 1, HALO : HALO + rows, :], load_sem.at[2])
-
-    pl.semaphore_wait(barrier, len(others))
+    own_rows = pl.ds(HALO, rows)
+    lanes = lax.broadcasted_iota(jnp.int32, (rows, LANES), 1)
+    outer = jnp.where(lanes < LANES // 2, fine[0, own_rows, :], fine[tiles - 1, own_rows, :])
+    outer = jnp.transpose(outer)
+    send_left[...] = outer[0:HALO, :]
+    send_right[...] = outer[LANES - HALO :, :]
+
+    pl.semaphore_wait(barrier, len(near))
 
     first_words = land.at[0:1, :]
     last_words = land.at[count_words - 1 : count_words, :]
@@ -163,28 +165,40 @@
         (first_words, right_words.at[:, own_lanes], (0, -1)),
         (last_words, left_words.at[:, own_lanes], (0, 1)),
     )
+    down_across_plan = (
+        (send_left.at[:, behind], right_side.at[:, top_lanes], (1, -1)),
+        (send_right.at[:, behind], left_side.at[:, top_lanes], (1, 1)),
+    )
+    down_words_plan = (
+        (first_words.at[:, behind], right_words.at[:, top_lanes], (1, -1)),
+        (last_words.at[:, behind], left_words.at[:, top_lanes], (1, 1)),
+    )
+    up_across_plan = (
+        (send_left.at[:, ahead], right_side.at[:, bottom_lanes], (-1, -1)),
+        (send_right.at[:, ahead], left_side.at[:, bottom_lanes], (-1, 1)),
+    )
+    up_words_plan = (
+        (first_words.at[:, ahead], right_words.at[:, bottom_lanes], (-1, -1)),
+        (last_words.at[:, ahead], left_words.at[:, bottom_lanes], (-1, 1)),
+    )
     down_plan = (
         (fine.at[:, rows : rows + HALO, :], fine.at[:, 0:HALO, :], (1, 0)),
         (words.at[rows : rows + HALO, :], words.at[0:HALO, :], (1, 0)),
-        (send_left.at[:, behind], right_side.at[:, top_lanes], (1, -1)),
-        (send_right.at[:, behind], left_side.at[:, top_lanes], (1, 1)),
-    )
-    down_words_plan = (
-        (first_words.at[:, behind], right_words.at[:, top_lanes], (1, -1)),
-        (last_words.at[:, behind], left_words.at[:, top_lanes], (1, 1)),
     )
     up_plan = (
         (fine.at[:, HALO : 2 * HALO, :], fine.at[:, HALO + rows :, :], (-1, 0)),
         (words.at[HALO : 2 * HALO, :], words.at[HALO + rows :, :], (-1, 0)),
-        (send_left.at[:, ahead], right_side.at[:, bottom_lanes], (-1, -1)),
-        (send_right.at[:, ahead], left_side.at[:, bottom_lanes], (-1, 1)),
-    )
-    up_words_plan = (
-        (first_words.at[:, ahead], right_words.at[:, bottom_lanes], (-1, -1)),
-        (last_words.at[:, ahead], left_words.at[:, bottom_lanes], (-1, 1)),
-    )
-    plans = (across_plan, down_plan, up_plan, down_words_plan, up_words_plan)
-    downs, ups = (1, 3), (2, 4)
+    )
+    plans = (
+        across_plan,
+        down_across_plan,
+        up_across_plan,
+        down_words_plan,
+        up_words_plan,
+        down_plan,
+        up_plan,
+    )
+    downs, ups = (1, 3, 5), (2, 4, 6)
 
     def settle_halo(which, sem):
         moved = sum(math.prod(source.shape) for source, _, _ in plans[which])
@@ -193,7 +207,7 @@
         else:
             settle(fine.at[0, 0 : moved // LANES, :], sem.at[which])
 
-    def copies(which):
+    def copies(which, taken):
         return [
             pltpu.make_async_remote_copy(
                 src_ref=source,
@@ -203,23 +217,57 @@
                 device_id=device(down, right),
                 device_id_type=MESH,
             )
-            for source, target, (down, right) in plans[which]
+            for source, target, (down, right) in plans[which][taken]
         ]
 
-    for copy in copies(0):
-        copy.start()
+    def send(which, taken=slice(None)):
+        for copy in copies(which, taken):
+            copy.start()
+
+    def send_side(side_at):
+        taken = slice(side_at, None, 2)
+        send(0, taken)
+
+        @pl.when(has_below)
+        def _():
+            send(1, taken)
+            send(3, taken)
+
+        @pl.when(has_above)
+        def _():
+            send(2, taken)
+            send(4, taken)
+
+    at_end = col_at == col_devices - 1
+    send_side(0)
+
+    @pl.when(at_end)
+    def _():
+        send_side(1)
+
+    @pl.when(jnp.logical_not(at_end))
+    def _():
+        send_side(1)
+
+    for right in range(1, col_devices):
+        pl.semaphore_signal(
+            column_sem, inc=1, device_id=device(0, right), device_id_type=MESH
+        )
+
+    settle(fine.at[1 : tiles - 1, HALO : HALO + rows, :], load_sem.at[2])
+    upright = land[...]
+    if count_words < LANES:
+        filler = jnp.zeros((LANES - count_words, rows), jnp.int32)
+        upright = jnp.concatenate([upright, filler], axis=0)
+    words[HALO : HALO + rows, :] = jnp.transpose(upright)
 
     @pl.when(has_below)
     def _():
-        for which in downs:
-            for copy in copies(which):
-                copy.start()
+        send(5)
 
     @pl.when(has_above)
     def _():
-        for which in ups:
-            for copy in copies(which):
-                copy.start()
+        send(6)
 
     blocks = rows // LANES + 2
     packed = cos_rows.shape
@@ -266,19 +314,21 @@
 
     sources = ((p0, c0), (p1, c1), (p2, c2), (p3, c3))
     splits = (split0, split1, split2, split3)
-    edges = (edge0, edge1, edge2, edge3)
     partials = (partial0, partial1, partial2, partial3)
     outputs = (level_one, level_two, level_three, level_four)
 
-    def downward(level, tile, first, count, target, at, stride):
-        lanes = pl.ds(tile * LANES, LANES)
-        for place, ref in enumerate(sources[level]):
+    def filtered(level, tile, first, count):
+        halves = []
+        for ref in sources[level]:
             taps = [ref[tile, pl.ds(7 + a + 2 * first, count, stride=2), :] for a in range(4)]
             down = (taps[0] + taps[3]) + 3.0 * (taps[1] + taps[2])
             high = down.astype(bf16)
-            low = (down - high.astype(f32)).astype(bf16)
-            target[pl.ds(2 * place * stride + at, count), lanes] = high
-            target[pl.ds((2 * place + 1) * stride + at, count), lanes] = low
+            halves += [high, (down - high.astype(f32)).astype(bf16)]
+        return halves
+
+    def downward(level, tile, first, count, target):
+        for place, half in enumerate(filtered(level, tile, first, count)):
+            target[place * count : (place + 1) * count, tile * LANES : (tile + 1) * LANES] = half
 
     def table(tap, keep=True):
         weight = jnp.where(
@@ -300,33 +350,37 @@
         return jnp.where(jnp.logical_or(at == half, at == half - 1), middle, away)
 
     lane_in = lax.broadcasted_iota(jnp.int32, (LANES, LANES), 0)
+    fine_in = jnp.where(
+        lane_in < half, lane_in % HALO, LANES - 1 - (LANES - 1 - lane_in) % HALO
+    )
     lane_out = lax.broadcasted_iota(jnp.int32, (LANES, LANES), 1)
     leftward = lane_out >= half
     from_side = table(
         column(lane_in) - 2 * column(lane_out) + 1, (lane_in >= half) == leftward
     )
+    from_side_fine = table(
+        column(fine_in) - 2 * column(lane_out) + 1, (lane_in >= half) == leftward
+    )
     from_first = table(lane_in - 2 * column(lane_out) + 1, leftward)
     from_last = table(lane_in - LANES - 2 * column(lane_out) + 1, jnp.logical_not(leftward))
-    last_and_side = jnp.concatenate([from_last, from_side], axis=0)
-
-    def across(source, count, parts):
+
+    def across(count, parts):
         result = None
-        for start, weights in parts:
-            part = jnp.dot(
-                source[0 : 4 * count, start * LANES : start * LANES + weights.shape[0]],
-                weights,
-                preferred_element_type=f32,
-            )
+        for operand, weights in parts:
+            part = jnp.dot(operand, weights, preferred_element_type=f32)
             result = part if result is None else result + part
         num = result[0:count] + result[count : 2 * count]
         den = result[2 * count : 3 * count] + result[3 * count :]
         return num, den
 
+    def window(level, start, stop):
+        return splits[level][:, start * LANES : stop * LANES]
+
     def own_parts(tile, tiles_in):
         start = max(2 * tile - 1, 0)
         stop = min(2 * tile + 3, tiles_in)
         skip = start - (2 * tile - 1)
-        return ((start, band[skip * LANES : (skip + stop - start) * LANES]),)
+        return start, stop, band[skip * LANES : (skip + stop - start) * LANES]
 
     def finish(num, den):
         value = num / jnp.maximum(den, floor_value)
@@ -375,13 +429,13 @@
     def inner_rows(level):
         return outputs[level].shape[0] + 16 - 2 * EDGE
 
-    def inner_tile(level, tile, num, den):
-        inner = inner_rows(level)
+    def inner_tile(level, tile, num, den, first=0):
+        inner = num.shape[0]
         value, cover, product = finish(num, den)
         cover, product, counted = masked(level, tile, value, cover, product)
         if level + 1 < LEVELS:
             for ref, array in zip(sources[level + 1], (product, cover)):
-                ref[tile, 16 + EDGE : 16 + EDGE + inner, :] = array
+                ref[tile, 16 + EDGE + first : 16 + EDGE + first + inner, :] = array
         stats[level] = tally(stats[level], *counted)
         return value
 
@@ -394,19 +448,23 @@
             if level == 0:
                 for start in range(0, rows, 64):
                     decode(tile, HALO + start, 64)
-            downward(level, tile, EDGE, inner, splits[level], 0, inner)
+            downward(level, tile, EDGE, inner, splits[level])
 
         fed = 0
         for tile in range(tiles_out):
             while fed < min(2 * tile + 3, tiles_in):
                 feed(fed)
                 fed += 1
-            value = inner_tile(
-                level, tile, *across(splits[level], inner, own_parts(tile, tiles_in))
-            )
+            start, stop, weights = own_parts(tile, tiles_in)
+            parts = ((window(level, start, stop), weights),)
+            value = inner_tile(level, tile, *across(inner, parts))
             lanes = slice(tile * LANES, (tile + 1) * LANES)
             outputs[level][EDGE - 8 : EDGE - 8 + inner, lanes] = value
-        num, den = across(splits[level], inner, ((0, from_first), (tiles_in - 1, from_last)))
+        parts = (
+            (window(level, 0, 1), from_first),
+            (window(level, tiles_in - 1, tiles_in), from_last),
+        )
+        num, den = across(inner, parts)
         partials[level][0] = num
         partials[level][1] = den
 
@@ -423,21 +481,28 @@
             settle_halo(which, halo_recv)
 
     sub = lax.broadcasted_iota(jnp.int32, (HALO, LANES), 0)
-    for block in range(blocks):
-        here = slice(block * LANES, (block + 1) * LANES)
-        turn = jnp.broadcast_to(cos_rows[block : block + 1, :], (HALO, LANES))
-        pieces = []
-        for index, (at, shift) in enumerate(((0, 0), (LANES - HALO, 32 - HALO))):
-            word = jnp.broadcast_to(side_words[index : index + 1, here], (HALO, LANES))
-            flag = jnp.bitwise_and(lax.shift_right_logical(word, sub + shift), 1)
-            cover = jnp.where(flag != 0, turn, 0.0)
-            pieces.append((cover, cover * side[at : at + HALO, here]))
-        filler = jnp.zeros((LANES - 2 * HALO, LANES), f32)
-        taken, at = placed(block)
-        size = taken.stop - taken.start
-        for kind, ref in ((0, c0), (1, p0)):
-            flat = jnp.concatenate([pieces[0][kind], filler, pieces[1][kind]], axis=0)
-            ref[tiles, 8 + at : 8 + at + size, :] = jnp.transpose(flat)[taken, :]
+    turned_lane = lax.broadcasted_iota(jnp.int32, (LANES, LANES), 1)
+    turned_slot = jnp.minimum(turned_lane, LANES - 1 - turned_lane) // HALO
+    filler = jnp.zeros((LANES - 8 * HALO, LANES), f32)
+    for pair in range(blocks // 2):
+        both = (pair, blocks - 1 - pair)
+        ends = ([], [])
+        for block in both:
+            here = slice(block * LANES, (block + 1) * LANES)
+            turn = jnp.broadcast_to(cos_rows[block : block + 1, :], (HALO, LANES))
+            for index, (at, shift) in enumerate(((0, 0), (LANES - HALO, 32 - HALO))):
+                word = jnp.broadcast_to(side_words[index : index + 1, here], (HALO, LANES))
+                flag = jnp.bitwise_and(lax.shift_right_logical(word, sub + shift), 1)
+                cover = jnp.where(flag != 0, turn, 0.0)
+                ends[index].extend((cover, cover * side[at : at + HALO, here]))
+        pieces = ends[0] + ([filler] if filler.shape[0] else []) + ends[1][::-1]
+        flat = jnp.transpose(jnp.concatenate(pieces, axis=0))
+        for index, block in enumerate(both):
+            taken, at = placed(block)
+            size = taken.stop - taken.start
+            for kind, ref in ((0, c0), (1, p0)):
+                held = jnp.where(turned_slot == 2 * index + kind, flat, 0.0)
+                ref[tiles, 8 + at : 8 + at + size, :] = held[taken, :]
 
     for tile in range(tiles):
         decode(tile, 0, HALO)
@@ -450,20 +515,33 @@
         own = output.shape[0]
         tiles_in = sources[level][0].shape[0] - 1
         tiles_out = output.shape[1] // LANES
-        downward(level, tiles_in, EDGE, inner, splits[level], 0, inner)
+        side_weights = from_side_fine if level == 0 else from_side
+        strips = []
         for tile in range(tiles_in + 1):
-            downward(level, tile, 0, EDGE, edges[level], 0, 2 * EDGE)
-            downward(level, tile, EDGE + inner, EDGE, edges[level], EDGE, 2 * EDGE)
-        num, den = across(splits[level], inner, ((tiles_in, from_side),))
-        inner_value = inner_tile(
-            level, tiles_out, num + partials[level][0], den + partials[level][1]
-        )
+            top = filtered(level, tile, 0, EDGE)
+            bottom = filtered(level, tile, EDGE + inner, EDGE)
+            pieces = [piece for pair in zip(top, bottom) for piece in pair]
+            strips.append(jnp.concatenate(pieces, axis=0))
+        inner_values = []
+        for first in range(0, inner, CHUNK):
+            count = min(CHUNK, inner - first)
+            operand = jnp.concatenate(filtered(level, tiles_in, EDGE + first, count), axis=0)
+            num, den = across(count, ((operand, side_weights),))
+            here = slice(first, first + count)
+            num, den = num + partials[level][0, here, :], den + partials[level][1, here, :]
+            inner_values.append(inner_tile(level, tiles_out, num, den, first))
+        inner_value = jnp.concatenate(inner_values, axis=0)
         for tile in range(tiles_out + 1):
             if tile == tiles_out:
-                parts = ((tiles_in - 1, last_and_side), (0, from_first))
+                parts = (
+                    (strips[tiles_in - 1], from_last),
+                    (strips[tiles_in], side_weights),
+                    (strips[0], from_first),
+                )
             else:
-                parts = own_parts(tile, tiles_in)
-            value, cover, product = finish(*across(edges[level], 2 * EDGE, parts))
+                start, stop, weights = own_parts(tile, tiles_in)
+                parts = ((jnp.concatenate(strips[start:stop], axis=1), weights),)
+            value, cover, product = finish(*across(2 * EDGE, parts))
             cover, product, counted = masked(level, tile, value, cover, product)
             if level + 1 < LEVELS:
                 for ref, array in zip(sources[level + 1], (product, cover)):
@@ -491,7 +569,9 @@
         largest = jnp.max(jnp.broadcast_to(largest, (8, LANES)), axis=1, keepdims=True)
         mine = jnp.where(lane == level, jnp.where(row < 2, sums, largest), mine)
     stat_own[...] = mine
-    for place, (down, right) in enumerate(others):
+    pl.semaphore_wait(column_sem, col_devices - 1)
+    far_first = sorted(enumerate(others), key=lambda other: (other[1][1] == 0, other[1][1]))
+    for place, (down, right) in far_first:
         copy = pltpu.make_async_remote_copy(
             src_ref=stat_own.at[0:4],
             dst_ref=stat_all.at[place, 0:4],
@@ -568,9 +648,7 @@
         scratch += [pltpu.VMEM(shape, f32)] * 2
     for level in range(LEVELS):
         inner = (rows >> (level + 1)) + 16 - 2 * EDGE
-        scratch.append(pltpu.VMEM((4 * inner, (cols >> level) + LANES), bf16))
-    for level in range(LEVELS):
-        scratch.append(pltpu.VMEM((8 * EDGE, (cols >> level) + LANES), bf16))
+        scratch.append(pltpu.VMEM((4 * inner, cols >> level), bf16))
     for level in range(LEVELS):
         inner = (rows >> (level + 1)) + 16 - 2 * EDGE
         scratch.append(pltpu.VMEM((2, inner, LANES), f32))
@@ -580,10 +658,11 @@
         pltpu.VMEM((others, 8, LANES), f32),
         pltpu.SemaphoreType.DMA((3,)),
         pltpu.SemaphoreType.DMA,
-        pltpu.SemaphoreType.DMA((5,)),
-        pltpu.SemaphoreType.DMA((5,)),
+        pltpu.SemaphoreType.DMA((7,)),
+        pltpu.SemaphoreType.DMA((7,)),
         pltpu.SemaphoreType.DMA,
         pltpu.SemaphoreType.DMA,
+        pltpu.SemaphoreType.REGULAR,
     ]
     vmem = pl.BlockSpec(memory_space=pltpu.VMEM)
     small = jax.ShapeDtypeStruct((LEVELS,), f32)

time: 20.2 us -> 19.1 us (0.946)
  Pallas kernels: 19.4 us -> 18.4 us
    pallas_call x1, Pallas kernels: 18.3 us -> 17.2 us  [per_device(): pl.pallas_call(functools.partial(kernel, row_devices, col_devices), out_s...]
where the time goes in v4:
time: 19.1 us; the launch traced here: 19 us
  Pallas kernels  18.4 us (96%)
  between operations  0.64 us (3%)
    pallas_call x1, Pallas kernels, per_device(): pl.pallas_call(functools.partial(kernel, row_devices, col_devices), out_s...  17.2 us
    pallas_call x1, Pallas kernels, per_device(): pl.pallas_call(hand_over, out_shape=results, in_specs=[vmem] * len(result...  1.12 us

profile of v4, /device:TPU:0, one launch (start us, length us, event | category | flops | bytes accessed | tf_op | source)
XLA Modules:
  0.0 19.0 jit_solution(14413242734572123320)
XLA Ops:
  0.6 17.2 %coarsen_levels.1 = (f32[256,1024]{1,0:T(8,128)S(1)}, f32[128,512]{1,0:T(8,128)S(1)}, f32[64,256]{1,0:T(8,128)S(1)}, f32[32,128]{1,0:T(8,128)S(1)}, f32[4]{0:T(128)S(1)}, /*index=5*/f32[4]{0:T(128)S(1)}) custom-call(f32[512,2048]{1,0:T(8,128)} %field.1, s32[64,512]{1,0:T(8,128)} %bitcast.1), custom_call_target="tpu_custom_call" | custom-call | tf_op jit(solution)/shard_map/coarsen_levels/pallas_call | solution.py:670
  17.9 1.1 %hand_over.1 = (f32[256,1024]{1,0:T(8,128)}, f32[128,512]{1,0:T(8,128)}, f32[64,256]{1,0:T(8,128)}, f32[32,128]{1,0:T(8,128)}, f32[4]{0:T(128)}, /*index=5*/f32[4]{0:T(128)}) custom-call(f32[256,1024]{1,0:T(8,128)S(1)} %get-tuple-element.12.refs_0_, f32[128,512]{1,0:T(8,128)S(1)} %get-tuple-element.13.refs_1_, f32[64,256]{1,0:T(8,128)S(1)} %get-tuple-element.14.refs_2_, ...), custom_call_target="tpu_custom_call" | custom-call | tf_op jit(solution)/shard_map/hand_over/pallas_call | solution.py:682

commit v5 on v4

--- a/solution.py
+++ b/solution.py
@@ -66,6 +66,8 @@
     stat_send,
     stat_recv,
     column_sem,
+    from_above_sem,
+    from_below_sem,
 ):
     rows, cols = field.shape
     tiles = cols // LANES
@@ -89,13 +91,8 @@
         if (down, right) != (0, 0)
     ]
 
-    near = [
-        (down, right)
-        for down, right in others
-        if down == 0
-        or right == 0
-        or (down in (1, row_devices - 1) and right in (1, col_devices - 1))
-    ]
+    near = [(down, right) for down, right in others if down == 0 or right == 0]
+
     land_load = pltpu.make_async_copy(land_words, land, land_sem)
 
     def load(tile):
@@ -145,6 +142,12 @@
     outer = jnp.transpose(outer)
     send_left[...] = outer[0:HALO, :]
     send_right[...] = outer[LANES - HALO :, :]
+
+    upright = land[...]
+    if count_words < LANES:
+        filler = jnp.zeros((LANES - count_words, rows), jnp.int32)
+        upright = jnp.concatenate([upright, filler], axis=0)
+    words[HALO : HALO + rows, :] = jnp.transpose(upright)
 
     pl.semaphore_wait(barrier, len(near))
 
@@ -224,9 +227,45 @@
         for copy in copies(which, taken):
             copy.start()
 
-    def send_side(side_at):
+    send(0, slice(0, None, 2))
+    send(0, slice(1, None, 2))
+
+    @pl.when(has_below)
+    def _():
+        pl.semaphore_signal(
+            from_above_sem, inc=1, device_id=device(1, 0), device_id_type=MESH
+        )
+
+    @pl.when(has_above)
+    def _():
+        pl.semaphore_signal(
+            from_below_sem, inc=1, device_id=device(-1, 0), device_id_type=MESH
+        )
+
+    for right in range(1, col_devices):
+        pl.semaphore_signal(
+            column_sem, inc=1, device_id=device(0, right), device_id_type=MESH
+        )
+
+    settle(fine.at[1 : tiles - 1, HALO : HALO + rows, :], load_sem.at[2])
+    @pl.when(has_below)
+    def _():
+        send(5)
+
+    @pl.when(has_above)
+    def _():
+        send(6)
+
+    @pl.when(has_below)
+    def _():
+        pl.semaphore_wait(from_below_sem, 1)
+
+    @pl.when(has_above)
+    def _():
+        pl.semaphore_wait(from_above_sem, 1)
+
+    for side_at in range(2):
         taken = slice(side_at, None, 2)
-        send(0, taken)
 
         @pl.when(has_below)
         def _():
@@ -237,37 +276,6 @@
         def _():
             send(2, taken)
             send(4, taken)
-
-    at_end = col_at == col_devices - 1
-    send_side(0)
-
-    @pl.when(at_end)
-    def _():
-        send_side(1)
-
-    @pl.when(jnp.logical_not(at_end))
-    def _():
-        send_side(1)
-
-    for right in range(1, col_devices):
-        pl.semaphore_signal(
-            column_sem, inc=1, device_id=device(0, right), device_id_type=MESH
-        )
-
-    settle(fine.at[1 : tiles - 1, HALO : HALO + rows, :], load_sem.at[2])
-    upright = land[...]
-    if count_words < LANES:
-        filler = jnp.zeros((LANES - count_words, rows), jnp.int32)
-        upright = jnp.concatenate([upright, filler], axis=0)
-    words[HALO : HALO + rows, :] = jnp.transpose(upright)
-
-    @pl.when(has_below)
-    def _():
-        send(5)
-
-    @pl.when(has_above)
-    def _():
-        send(6)
 
     blocks = rows // LANES + 2
     packed = cos_rows.shape
@@ -468,17 +476,25 @@
         partials[level][0] = num
         partials[level][1] = den
 
+    @pl.when(has_below)
+    def _():
+        settle_halo(6, halo_recv)
+
+    @pl.when(has_above)
+    def _():
+        settle_halo(5, halo_recv)
+
     settle_halo(0, halo_recv)
 
     @pl.when(has_below)
     def _():
-        for which in ups:
-            settle_halo(which, halo_recv)
+        settle_halo(2, halo_recv)
+        settle_halo(4, halo_recv)
 
     @pl.when(has_above)
     def _():
-        for which in downs:
-            settle_halo(which, halo_recv)
+        settle_halo(1, halo_recv)
+        settle_halo(3, halo_recv)
 
     sub = lax.broadcasted_iota(jnp.int32, (HALO, LANES), 0)
     turned_lane = lax.broadcasted_iota(jnp.int32, (LANES, LANES), 1)
@@ -508,55 +524,68 @@
         decode(tile, 0, HALO)
         decode(tile, HALO + rows, HALO)
 
+    def keep_strip(level, tile, cover, product):
+        inner = inner_rows(level)
+        own = outputs[level].shape[0]
+        if level + 1 < LEVELS:
+            for ref, array in zip(sources[level + 1], (product, cover)):
+                ref[tile, 16:24, :] = array[0:8] * above_factor
+                ref[tile, 24 : 16 + EDGE, :] = array[8:EDGE]
+                ref[tile, 16 + EDGE + inner : 24 + own, :] = array[EDGE : 2 * EDGE - 8]
+                ref[tile, 24 + own : 32 + own, :] = array[2 * EDGE - 8 :] * below_factor
+
+    def strip(level, tile):
+        top = filtered(level, tile, 0, EDGE)
+        bottom = filtered(level, tile, EDGE + inner_rows(level), EDGE)
+        return [piece for pair in zip(top, bottom) for piece in pair]
+
+    middle = slice(8, 2 * EDGE - 8)
+    def across_side(level, halves):
+        weights = from_side_fine if level == 0 else from_side
+        weights = jnp.concatenate([weights, weights], axis=0)
+        high = jnp.concatenate(halves[0 : len(halves) // 4] + halves[len(halves) // 2 : -(len(halves) // 4)], axis=0)
+        low = jnp.concatenate(halves[len(halves) // 4 : len(halves) // 2] + halves[-(len(halves) // 4) :], axis=0)
+        count = high.shape[0] // 2
+        result = jnp.dot(
+            jnp.concatenate([high, low], axis=1), weights, preferred_element_type=f32
+        )
+        return result[0:count], result[count:]
+
     ring_values = []
     for level in range(LEVELS):
-        inner = inner_rows(level)
         output = outputs[level]
         own = output.shape[0]
         tiles_in = sources[level][0].shape[0] - 1
         tiles_out = output.shape[1] // LANES
-        side_weights = from_side_fine if level == 0 else from_side
-        strips = []
-        for tile in range(tiles_in + 1):
-            top = filtered(level, tile, 0, EDGE)
-            bottom = filtered(level, tile, EDGE + inner, EDGE)
-            pieces = [piece for pair in zip(top, bottom) for piece in pair]
-            strips.append(jnp.concatenate(pieces, axis=0))
+        strips = [jnp.concatenate(strip(level, tile), axis=0) for tile in range(tiles_in)]
+        for tile in range(tiles_out):
+            start, stop, weights = own_parts(tile, tiles_in)
+            parts = ((jnp.concatenate(strips[start:stop], axis=1), weights),)
+            value, cover, product = finish(*across(2 * EDGE, parts))
+            cover, product, counted = masked(level, tile, value, cover, product)
+            keep_strip(level, tile, cover, product)
+            stats[level] = tally(stats[level], *(array[middle] for array in counted))
+            lanes = slice(tile * LANES, (tile + 1) * LANES)
+            output[0 : EDGE - 8, lanes] = value[8:EDGE]
+            output[own - EDGE + 8 :, lanes] = value[EDGE : 2 * EDGE - 8]
+        parts = ((strips[tiles_in - 1], from_last), (strips[0], from_first))
+        edge_partial = across(2 * EDGE, parts)
+        inner = inner_rows(level)
         inner_values = []
         for first in range(0, inner, CHUNK):
             count = min(CHUNK, inner - first)
-            operand = jnp.concatenate(filtered(level, tiles_in, EDGE + first, count), axis=0)
-            num, den = across(count, ((operand, side_weights),))
+            num, den = across_side(level, filtered(level, tiles_in, EDGE + first, count))
             here = slice(first, first + count)
             num, den = num + partials[level][0, here, :], den + partials[level][1, here, :]
             inner_values.append(inner_tile(level, tiles_out, num, den, first))
         inner_value = jnp.concatenate(inner_values, axis=0)
-        for tile in range(tiles_out + 1):
-            if tile == tiles_out:
-                parts = (
-                    (strips[tiles_in - 1], from_last),
-                    (strips[tiles_in], side_weights),
-                    (strips[0], from_first),
-                )
-            else:
-                start, stop, weights = own_parts(tile, tiles_in)
-                parts = ((jnp.concatenate(strips[start:stop], axis=1), weights),)
-            value, cover, product = finish(*across(2 * EDGE, parts))
-            cover, product, counted = masked(level, tile, value, cover, product)
-            if level + 1 < LEVELS:
-                for ref, array in zip(sources[level + 1], (product, cover)):
-                    ref[tile, 16:24, :] = array[0:8] * above_factor
-                    ref[tile, 24 : 16 + EDGE, :] = array[8:EDGE]
-                    ref[tile, 16 + EDGE + inner : 24 + own, :] = array[EDGE : 2 * EDGE - 8]
-                    ref[tile, 24 + own : 32 + own, :] = array[2 * EDGE - 8 :] * below_factor
-            middle = slice(8, 2 * EDGE - 8)
-            stats[level] = tally(stats[level], *(array[middle] for array in counted))
-            if tile < tiles_out:
-                lanes = slice(tile * LANES, (tile + 1) * LANES)
-                output[0 : EDGE - 8, lanes] = value[8:EDGE]
-                output[own - EDGE + 8 :, lanes] = value[EDGE : 2 * EDGE - 8]
-            else:
-                ring_values.append((inner_value, value[middle]))
+        num, den = across_side(level, strip(level, tiles_in))
+        num, den = num + edge_partial[0], den + edge_partial[1]
+        value, cover, product = finish(num, den)
+        cover, product, counted = masked(level, tiles_out, value, cover, product)
+        keep_strip(level, tiles_out, cover, product)
+        stats[level] = tally(stats[level], *(array[middle] for array in counted))
+        ring_values.append((inner_value, value[middle]))
 
     lane = lax.broadcasted_iota(jnp.int32, (8, LANES), 1)
     row = lax.broadcasted_iota(jnp.int32, (8, LANES), 0)
@@ -663,6 +692,8 @@
         pltpu.SemaphoreType.DMA,
         pltpu.SemaphoreType.DMA,
         pltpu.SemaphoreType.REGULAR,
+        pltpu.SemaphoreType.REGULAR,
+        pltpu.SemaphoreType.REGULAR,
     ]
     vmem = pl.BlockSpec(memory_space=pltpu.VMEM)
     small = jax.ShapeDtypeStruct((LEVELS,), f32)

time: 19.1 us -> 18.8 us (0.984)
  Pallas kernels: 18.4 us -> 18.1 us
    pallas_call x1, Pallas kernels: 17.2 us -> 16.9 us  [per_device(): pl.pallas_call(functools.partial(kernel, row_devices, col_devices), out_s...]
where the time goes in v5:
time: 18.8 us; the launch traced here: 18.7 us
  Pallas kernels  18.1 us (96%)
  between operations  0.64 us (3%)
    pallas_call x1, Pallas kernels, per_device(): pl.pallas_call(functools.partial(kernel, row_devices, col_devices), out_s...  16.9 us
    pallas_call x1, Pallas kernels, per_device(): pl.pallas_call(hand_over, out_shape=results, in_specs=[vmem] * len(result...  1.12 us

profile of v5, /device:TPU:0, one launch (start us, length us, event | category | flops | bytes accessed | tf_op | source)
XLA Modules:
  0.0 18.7 jit_solution(8726146955830671601)
XLA Ops:
  0.6 16.9 %coarsen_levels.1 = (f32[256,1024]{1,0:T(8,128)S(1)}, f32[128,512]{1,0:T(8,128)S(1)}, f32[64,256]{1,0:T(8,128)S(1)}, f32[32,128]{1,0:T(8,128)S(1)}, f32[4]{0:T(128)S(1)}, /*index=5*/f32[4]{0:T(128)S(1)}) custom-call(f32[512,2048]{1,0:T(8,128)} %field.1, s32[64,512]{1,0:T(8,128)} %bitcast.1), custom_call_target="tpu_custom_call" | custom-call | tf_op jit(solution)/shard_map/coarsen_levels/pallas_call | solution.py:701
  17.6 1.1 %hand_over.1 = (f32[256,1024]{1,0:T(8,128)}, f32[128,512]{1,0:T(8,128)}, f32[64,256]{1,0:T(8,128)}, f32[32,128]{1,0:T(8,128)}, f32[4]{0:T(128)}, /*index=5*/f32[4]{0:T(128)}) custom-call(f32[256,1024]{1,0:T(8,128)S(1)} %get-tuple-element.12.refs_0_, f32[128,512]{1,0:T(8,128)S(1)} %get-tuple-element.13.refs_1_, f32[64,256]{1,0:T(8,128)S(1)} %get-tuple-element.14.refs_2_, ...), custom_call_target="tpu_custom_call" | custom-call | tf_op jit(solution)/shard_map/hand_over/pallas_call | solution.py:713

commit v6 on v5

--- a/solution.py
+++ b/solution.py
@@ -49,10 +49,6 @@
     c2,
     p3,
     c3,
-    split0,
-    split1,
-    split2,
-    split3,
     partial0,
     partial1,
     partial2,
@@ -321,7 +317,6 @@
         p0[tile, pl.ds(8 + start, count), :] = cover * fine[tile, pl.ds(start, count), :]
 
     sources = ((p0, c0), (p1, c1), (p2, c2), (p3, c3))
-    splits = (split0, split1, split2, split3)
     partials = (partial0, partial1, partial2, partial3)
     outputs = (level_one, level_two, level_three, level_four)
 
@@ -334,10 +329,6 @@
             halves += [high, (down - high.astype(f32)).astype(bf16)]
         return halves
 
-    def downward(level, tile, first, count, target):
-        for place, half in enumerate(filtered(level, tile, first, count)):
-            target[place * count : (place + 1) * count, tile * LANES : (tile + 1) * LANES] = half
-
     def table(tap, keep=True):
         weight = jnp.where(
             jnp.logical_or(tap == 0, tap == 3),
@@ -380,9 +371,6 @@
         num = result[0:count] + result[count : 2 * count]
         den = result[2 * count : 3 * count] + result[3 * count :]
         return num, den
-
-    def window(level, start, stop):
-        return splits[level][:, start * LANES : stop * LANES]
 
     def own_parts(tile, tiles_in):
         start = max(2 * tile - 1, 0)
@@ -456,21 +444,22 @@
             if level == 0:
                 for start in range(0, rows, 64):
                     decode(tile, HALO + start, 64)
-            downward(level, tile, EDGE, inner, splits[level])
-
+            operands.append(jnp.concatenate(filtered(level, tile, EDGE, inner), axis=0))
+
+        operands = []
         fed = 0
         for tile in range(tiles_out):
             while fed < min(2 * tile + 3, tiles_in):
                 feed(fed)
                 fed += 1
             start, stop, weights = own_parts(tile, tiles_in)
-            parts = ((window(level, start, stop), weights),)
+            parts = ((jnp.concatenate(operands[start:stop], axis=1), weights),)
             value = inner_tile(level, tile, *across(inner, parts))
             lanes = slice(tile * LANES, (tile + 1) * LANES)
             outputs[level][EDGE - 8 : EDGE - 8 + inner, lanes] = value
         parts = (
-            (window(level, 0, 1), from_first),
-            (window(level, tiles_in - 1, tiles_in), from_last),
+            (operands[0], from_first),
+            (operands[tiles_in - 1], from_last),
         )
         num, den = across(inner, parts)
         partials[level][0] = num
@@ -677,9 +666,6 @@
         scratch += [pltpu.VMEM(shape, f32)] * 2
     for level in range(LEVELS):
         inner = (rows >> (level + 1)) + 16 - 2 * EDGE
-        scratch.append(pltpu.VMEM((4 * inner, cols >> level), bf16))
-    for level in range(LEVELS):
-        inner = (rows >> (level + 1)) + 16 - 2 * EDGE
         scratch.append(pltpu.VMEM((2, inner, LANES), f32))
     others = row_devices * col_devices - 1
     scratch += [

time: 18.8 us -> 18.6 us (0.989)
  Pallas kernels: 18.1 us -> 17.8 us
    pallas_call x1, Pallas kernels: 16.9 us -> 16.7 us  [per_device(): pl.pallas_call(functools.partial(kernel, row_devices, col_devices), out_s...]
where the time goes in v6:
time: 18.6 us; the launch traced here: 18.4 us
  Pallas kernels  17.8 us (96%)
  between operations  0.64 us (3%)
    pallas_call x1, Pallas kernels, per_device(): pl.pallas_call(functools.partial(kernel, row_devices, col_devices), out_s...  16.7 us
    pallas_call x1, Pallas kernels, per_device(): pl.pallas_call(hand_over, out_shape=results, in_specs=[vmem] * len(result...  1.12 us

profile of v6, /device:TPU:0, one launch (start us, length us, event | category | flops | bytes accessed | tf_op | source)
XLA Modules:
  0.0 18.4 jit_solution(6475294050307380396)
XLA Ops:
  0.6 16.7 %coarsen_levels.1 = (f32[256,1024]{1,0:T(8,128)S(1)}, f32[128,512]{1,0:T(8,128)S(1)}, f32[64,256]{1,0:T(8,128)S(1)}, f32[32,128]{1,0:T(8,128)S(1)}, f32[4]{0:T(128)S(1)}, /*index=5*/f32[4]{0:T(128)S(1)}) custom-call(f32[512,2048]{1,0:T(8,128)} %field.1, s32[64,512]{1,0:T(8,128)} %bitcast.1), custom_call_target="tpu_custom_call" | custom-call | tf_op jit(solution)/shard_map/coarsen_levels/pallas_call | solution.py:687
  17.3 1.1 %hand_over.1 = (f32[256,1024]{1,0:T(8,128)}, f32[128,512]{1,0:T(8,128)}, f32[64,256]{1,0:T(8,128)}, f32[32,128]{1,0:T(8,128)}, f32[4]{0:T(128)}, /*index=5*/f32[4]{0:T(128)}) custom-call(f32[256,1024]{1,0:T(8,128)S(1)} %get-tuple-element.12.refs_0_, f32[128,512]{1,0:T(8,128)S(1)} %get-tuple-element.13.refs_1_, f32[64,256]{1,0:T(8,128)S(1)} %get-tuple-element.14.refs_2_, ...), custom_call_target="tpu_custom_call" | custom-call | tf_op jit(solution)/shard_map/hand_over/pallas_call | solution.py:699

commit v7 on v6

--- a/solution.py
+++ b/solution.py
@@ -588,17 +588,25 @@
         mine = jnp.where(lane == level, jnp.where(row < 2, sums, largest), mine)
     stat_own[...] = mine
     pl.semaphore_wait(column_sem, col_devices - 1)
-    far_first = sorted(enumerate(others), key=lambda other: (other[1][1] == 0, other[1][1]))
-    for place, (down, right) in far_first:
-        copy = pltpu.make_async_remote_copy(
-            src_ref=stat_own.at[0:4],
-            dst_ref=stat_all.at[place, 0:4],
-            send_sem=stat_send,
-            recv_sem=stat_recv,
-            device_id=device(down, right),
-            device_id_type=MESH,
-        )
-        copy.start()
+    def send_stats(sign):
+        order = sorted(enumerate(others), key=lambda other: (other[1][1] == 0, sign * other[1][1]))
+        for place, (down, right) in order:
+            pltpu.make_async_remote_copy(
+                src_ref=stat_own.at[0:4],
+                dst_ref=stat_all.at[place, 0:4],
+                send_sem=stat_send,
+                recv_sem=stat_recv,
+                device_id=device(down, right),
+                device_id_type=MESH,
+            ).start()
+
+    @pl.when(2 * col_at < col_devices)
+    def _():
+        send_stats(-1)
+
+    @pl.when(2 * col_at >= col_devices)
+    def _():
+        send_stats(1)
 
     for output, (inner_value, edge_value) in zip(outputs, ring_values):
         own, width = output.shape

time: 18.6 us -> 18.6 us (level)
  no operation moved by 1% of the time
where the time goes in v7:
time: 18.6 us; the launch traced here: 18.4 us
  Pallas kernels  17.8 us (96%)
  between operations  0.64 us (3%)
    pallas_call x1, Pallas kernels, per_device(): pl.pallas_call(functools.partial(kernel, row_devices, col_devices), out_s...  16.7 us
    pallas_call x1, Pallas kernels, per_device(): pl.pallas_call(hand_over, out_shape=results, in_specs=[vmem] * len(result...  1.12 us

profile of v7, /device:TPU:0, one launch (start us, length us, event | category | flops | bytes accessed | tf_op | source)
XLA Modules:
  0.0 18.4 jit_solution(8911010434902946891)
XLA Ops:
  0.6 16.7 %coarsen_levels.1 = (f32[256,1024]{1,0:T(8,128)S(1)}, f32[128,512]{1,0:T(8,128)S(1)}, f32[64,256]{1,0:T(8,128)S(1)}, f32[32,128]{1,0:T(8,128)S(1)}, f32[4]{0:T(128)S(1)}, /*index=5*/f32[4]{0:T(128)S(1)}) custom-call(f32[512,2048]{1,0:T(8,128)} %field.1, s32[64,512]{1,0:T(8,128)} %bitcast.1), custom_call_target="tpu_custom_call" | custom-call | tf_op jit(solution)/shard_map/coarsen_levels/pallas_call | solution.py:695
  17.3 1.1 %hand_over.1 = (f32[256,1024]{1,0:T(8,128)}, f32[128,512]{1,0:T(8,128)}, f32[64,256]{1,0:T(8,128)}, f32[32,128]{1,0:T(8,128)}, f32[4]{0:T(128)}, /*index=5*/f32[4]{0:T(128)}) custom-call(f32[256,1024]{1,0:T(8,128)S(1)} %get-tuple-element.12.refs_0_, f32[128,512]{1,0:T(8,128)S(1)} %get-tuple-element.13.refs_1_, f32[64,256]{1,0:T(8,128)S(1)} %get-tuple-element.14.refs_2_, ...), custom_call_target="tpu_custom_call" | custom-call | tf_op jit(solution)/shard_map/hand_over/pallas_call | solution.py:707
